TPU v7x, 32 devices: a whole 2x2x4 slice. The times are simulated.
32 devices in a mesh: fft: 16 (over z, x, core), scal: 2 (over y).
Axes of the slice: x: 2, y: 2, z: 4, core: 2. Of those that a mesh axis runs over, the one named last changes fastest.
Arguments:
- scalar_state: float32 [2, 2, 256, 256, 128], P('scal', None, 'fft'), may hold values from -12 to 12
- velocity: bfloat16 [3, 256, 256, 256], P(None, 'fft', 'scal'), may hold values from -6 to 6
- species: int32 [2], P('scal'), may hold values from 0 to 63
- kappa_table: float32 [64], replicated, may hold values from 0.1 to 1
- dealias_bound: int32 [2], P('scal'), may hold values from 64 to 85
Outputs:
- new_state: float32 [2, 2, 256, 256, 128], P('scal', None, 'fft')
- kappa: float32 [2], P('scal')
All inputs are finite; a program needn't handle non-finite values.
Results may differ from a plain program's by a relative error of at most 0.0027.
Values may be sent and summed in bfloat16 or wider, within the bound.
A program may use at most 128 MiB of HBM per device.

v0:
```python
import functools
import math

import numpy as np

import jax
import jax.numpy as jnp
from jax import lax
from jax.experimental import pallas as pl
from jax.experimental.pallas import tpu as pltpu
from jax.sharding import PartitionSpec as P

MESH = pl.DeviceIdType.MESH
cfl_number = 0.2


def twiddle(size_in, size_out, length):
    row_index = np.arange(size_in, dtype=np.int32)[:, None]
    col_index = np.arange(size_out, dtype=np.int32)[None, :]
    angles = (row_index * col_index % length).astype(np.float32) * np.float32(2.0 * math.pi / length)
    norming = np.float32(1.0 / math.sqrt(length))
    return (np.cos(angles) * norming, np.sin(angles) * norming)


def build_tables(length):
    half = length // 2
    quarter = half // 4
    full_cos, full_sin = twiddle(length, length, length)
    inv_cos, inv_sin = twiddle(half, length, length)
    weight = np.where(np.arange(half) == 0, 1.0, 2.0).astype(np.float32)[:, None]
    fwd_cos, fwd_sin = twiddle(length, half, length)
    inv_y = np.block([[full_cos, -full_sin], [full_sin, full_cos]])
    inv_x = np.concatenate([inv_cos * weight, -inv_sin * weight], axis=0)
    orders = [
        np.concatenate([((p - l - 1) % 4) * quarter + np.arange(quarter) for l in range(4)]) for p in range(4)
    ]
    fwd_x = np.stack([np.concatenate([fwd_cos[:, o], -fwd_sin[:, o]], axis=1) for o in orders])
    return tuple(jnp.asarray(t.astype(np.float32).astype(jnp.bfloat16)) for t in (inv_y, inv_x, fwd_x))


def dot(a, b):
    return jnp.dot(a, b, preferred_element_type=jnp.float32)


def stage_kernel(n, m, rows, chunk, band, first, *refs):
    if first:
        (send, vel, stat_in, inv_y, inv_x, fwd_x, fwd_y,
         gout, uall, stat_out,
         recv, fsend, raw, packed, peak, stat, s_send, s_recv, f_send, f_recv, l_sem, u_send, u_recv, u_loc,
         t_send, t_recv, t_loc) = refs
    else:
        (send, uall, inv_y, inv_x, fwd_x, fwd_y,
         gout,
         recv, fsend, raw, packed, s_send, s_recv, f_send, f_recv, l_sem) = refs
    length = n * rows
    half = length // 2
    count = rows // chunk
    me = lax.axis_index("fft")
    mine = lax.axis_index("scal")

    groups = rows // 4
    quarter = half // 4

    def needed(d, t):
        low = d * rows
        least = jnp.where(low < half, low, length - low - rows + 1)
        return (t * quarter) ** 2 + least * least <= band * band

    def by_tiles(d, act):
        for k in range(1, 4):
            wanted = needed(d, k - 1)
            if k < 3:
                wanted = jnp.logical_and(wanted, jnp.logical_not(needed(d, k)))

            @pl.when(wanted)
            def _():
                act(k)

    barrier = pltpu.get_barrier_semaphore()

    def greet(j, carry):
        pl.semaphore_signal(barrier, inc=1, device_id={"fft": lax.rem(me + j, n)}, device_id_type=MESH)
        return carry

    lax.fori_loop(1, n, greet, 0)
    if first:
        def greet_other(j, carry):
            pl.semaphore_signal(
                barrier, inc=1, device_id={"scal": lax.rem(mine + j, m)}, device_id_type=MESH
            )
            return carry

        lax.fori_loop(1, m, greet_other, 0)
        pl.semaphore_wait(barrier, n + m - 2)
    else:
        pl.semaphore_wait(barrier, n - 1)

    def inverse_copy(c, d, slot):
        return pltpu.make_async_remote_copy(
            src_ref=send.at[:, d, pl.ds(c * chunk, chunk)],
            dst_ref=recv.at[:, pl.ds(c * chunk, chunk), slot],
            send_sem=s_send.at[c, d],
            recv_sem=s_recv.at[c, slot],
            device_id={"fft": d},
            device_id_type=MESH,
        )

    def own_copy(c):
        return pltpu.make_async_copy(
            send.at[:, me, pl.ds(c * chunk, chunk)], recv.at[:, pl.ds(c * chunk, chunk), me], l_sem.at[0, c]
        )

    def speed_copy(c, s, slot):
        return pltpu.make_async_remote_copy(
            src_ref=vel.at[:, pl.ds(c * chunk, chunk)],
            dst_ref=uall.at[:, pl.ds(c * chunk, chunk), slot],
            send_sem=u_send.at[c, s],
            recv_sem=u_recv.at[c, slot],
            device_id={"scal": s},
            device_id_type=MESH,
        )

    def own_speed(c):
        return pltpu.make_async_copy(
            vel.at[:, pl.ds(c * chunk, chunk)], uall.at[:, pl.ds(c * chunk, chunk), mine], u_loc.at[c]
        )

    def forward_copy(g, d, slot, k):
        return pltpu.make_async_remote_copy(
            src_ref=fsend.at[d, g, pl.ds(0, k)],
            dst_ref=raw.at[slot, g, pl.ds(0, k)],
            send_sem=f_send.at[g, d],
            recv_sem=f_recv.at[g, slot],
            device_id={"fft": d},
            device_id_type=MESH,
        )

    def own_forward(g):
        return pltpu.make_async_copy(fsend.at[me, g], raw.at[me, g], l_sem.at[1, g])

    def stat_copy(d, slot):
        return pltpu.make_async_remote_copy(
            src_ref=stat,
            dst_ref=stat_out.at[slot],
            send_sem=t_send.at[d],
            recv_sem=t_recv.at[slot],
            device_id={"fft": d},
            device_id_type=MESH,
        )

    def start_chunk(c, carry):
        def one(j, inner):
            inverse_copy(c, lax.rem(me + j, n), me).start()
            return inner

        lax.fori_loop(1, n, one, 0)
        own_copy(c).start()
        if first:
            def two(j, inner):
                speed_copy(c, lax.rem(mine + j, m), mine).start()
                return inner

            lax.fori_loop(1, m, two, 0)
            own_speed(c).start()
        return carry

    lax.fori_loop(0, count, start_chunk, 0)

    if first:
        peak[...] = jnp.zeros_like(peak)

    for t in range(3):
        @pl.when(jnp.logical_not(needed(me, t)))
        def _():
            def clear(j, carry):
                raw[lax.rem(me + j, n), :, t] = jnp.zeros((groups, 2, rows, half), jnp.bfloat16)
                return carry

            lax.fori_loop(1, n, clear, 0)

    row = lax.broadcasted_iota(jnp.int32, (length, half), 0)
    ky = jnp.where(row < half, row, row - length).astype(jnp.float32)
    kx = lax.broadcasted_iota(jnp.int32, (length, half), 1).astype(jnp.float32)

    lane = lax.broadcasted_iota(jnp.int32, (2 * length, half), 1) // quarter

    def pick(choices):
        result = choices[-1]
        for i in range(len(choices) - 2, -1, -1):
            result = jnp.where(lane == i, choices[i], result)
        return result

    def pair(z, h):
        parts = []
        for p in range(2):
            block = jnp.concatenate([recv[q, z + p].reshape(length, 2 * half) for q in range(2)], axis=0)
            w_real = block[:length, :half].astype(jnp.float32)
            w_imag = block[length:, :half].astype(jnp.float32)
            turned = jnp.concatenate(
                [(-ky * w_imag).astype(jnp.bfloat16), (ky * w_real).astype(jnp.bfloat16)], axis=0
            )
            parts += [block, turned]
        section = dot(inv_y[...], jnp.concatenate(parts, axis=1))
        halves = []
        for p in range(2):
            at = 3 * half * p
            w_real = section[:length, at : at + half]
            w_imag = section[length:, at : at + half]
            sides = [
                (-kx * w_imag, kx * w_real),
                (section[:length, at + 2 * half : at + 3 * half], section[length:, at + 2 * half : at + 3 * half]),
                (section[:length, at + half : at + 2 * half], section[length:, at + half : at + 2 * half]),
            ]
            total = None
            square = None
            for i, (re, im) in enumerate(sides):
                lhs = jnp.concatenate([re.astype(jnp.bfloat16), im.astype(jnp.bfloat16)], axis=1)
                grad = dot(lhs, inv_x[...])
                u = uall[i, z + p].reshape(length, length).astype(jnp.float32)
                total = u * grad if total is None else total + u * grad
                if first:
                    square = grad * grad if square is None else square + grad * grad
            if first:
                peak[...] = jnp.maximum(peak[...], jnp.max(square.reshape(length // 8, 8, length), axis=0))
            flat = dot(total.astype(jnp.bfloat16), fwd_x[2 * h + p]).astype(jnp.bfloat16)
            halves.append(jnp.concatenate([flat[:, :half], flat[:, half:]], axis=0))
        packed[h] = dot(fwd_y[...], jnp.concatenate(halves, axis=1))

    def run_group(g, carry):
        def one_pair(h, outer):
            c = 2 * g + h

            def arrive(j, inner):
                inverse_copy(c, lax.rem(me + j, n), lax.rem(me + n - j, n)).wait_recv()
                return inner

            lax.fori_loop(1, n, arrive, 0)
            own_copy(c).wait()
            if first:
                def arrive_speed(j, inner):
                    speed_copy(c, lax.rem(mine + j, m), lax.rem(mine + m - j, m)).wait_recv()
                    return inner

                lax.fori_loop(1, m, arrive_speed, 0)
                own_speed(c).wait()
            pair(c * chunk, h)
            return outer

        lax.fori_loop(0, 2, one_pair, 0)

        for t in range(3):
            chosen = [(i + 1 + t) % 4 for i in range(4)]
            tile = pick([packed[p // 2, :, (p % 2) * half : (p % 2 + 1) * half] for p in chosen])
            tile = tile.astype(jnp.bfloat16)
            for q in range(2):
                fsend[:, g, t, q] = tile[q * length : (q + 1) * length].reshape(n, rows, half)

        def leave(j, inner):
            d = lax.rem(me + j, n)
            by_tiles(d, lambda k: forward_copy(g, d, me, k).start())
            return inner

        lax.fori_loop(1, n, leave, 0)
        own_forward(g).start()
        return carry

    lax.fori_loop(0, groups, run_group, 0)

    if first:
        line = lax.broadcasted_iota(jnp.int32, stat.shape, 0)
        largest = jnp.sqrt(jnp.max(peak[...], keepdims=True))
        stat[...] = jnp.where(line == 2, largest, stat_in[...])

        def tell(j, carry):
            stat_copy(lax.rem(me + j, n), me).start()
            return carry

        lax.fori_loop(1, n, tell, 0)
        pltpu.make_async_copy(stat, stat_out.at[me], t_loc).start()

    def unpack(g, carry):
        def one(j, inner):
            d = lax.rem(me + j, n)
            by_tiles(me, lambda k: forward_copy(g, d, lax.rem(me + n - j, n), k).wait_recv())
            return inner

        lax.fori_loop(1, n, one, 0)
        own_forward(g).wait()
        tiles = [raw[:, g, t].reshape(2 * length, half).astype(jnp.float32) for t in range(3)]
        for p in range(4):
            moved = [
                pltpu.roll(tiles[t], (2 * t + 1 - p) % 4 * quarter, 1) if (2 * t + 1 - p) % 4 else tiles[t]
                for t in range(3)
            ]
            plane = pick(moved + [jnp.zeros_like(tiles[0])]).astype(jnp.bfloat16).reshape(n, 2, rows, half)
            for q in range(2):
                gout[q, :, 4 * g + p] = plane[:, q]
        return carry

    lax.fori_loop(0, groups, unpack, 0)

    def finish(c, carry):
        def one(j, inner):
            inverse_copy(c, lax.rem(me + j, n), me).wait_send()
            return inner

        lax.fori_loop(1, n, one, 0)
        if first:
            def two(j, inner):
                speed_copy(c, lax.rem(mine + j, m), mine).wait_send()
                return inner

            lax.fori_loop(1, m, two, 0)
        return carry

    lax.fori_loop(0, count, finish, 0)

    def finish_forward(g, carry):
        def one(j, inner):
            d = lax.rem(me + j, n)
            by_tiles(d, lambda k: forward_copy(g, d, me, k).wait_send())
            return inner

        lax.fori_loop(1, n, one, 0)
        return carry

    lax.fori_loop(0, groups, finish_forward, 0)

    if first:
        def told(j, carry):
            stat_copy(lax.rem(me + j, n), me).wait_send()
            stat_copy(lax.rem(me + j, n), lax.rem(me + n - j, n)).wait_recv()
            return carry

        lax.fori_loop(1, n, told, 0)
        pltpu.make_async_copy(stat, stat_out.at[me], t_loc).wait()


def run_stage(n, m, rows, first, send, speeds, tables, stat_in=None):
    length = n * rows
    half = length // 2
    chunk = 2
    count = rows // chunk
    groups = rows // 4
    band = length // 3
    vmem = pl.BlockSpec(memory_space=pltpu.VMEM)
    hbm = pl.BlockSpec(memory_space=pl.ANY)
    dma = pltpu.SemaphoreType.DMA
    out_shape = [jax.ShapeDtypeStruct((2, n, rows, rows, half), jnp.bfloat16)]
    scratch = [
        pltpu.VMEM((2, rows, n, rows, 2 * half), jnp.bfloat16),
        pltpu.VMEM((n, groups, 3, 2, rows, half), jnp.bfloat16),
        pltpu.VMEM((n, groups, 3, 2, rows, half), jnp.bfloat16),
        pltpu.VMEM((2, 2 * length, 2 * half), jnp.float32),
    ]
    sems = [dma((count, n)), dma((count, n)), dma((groups, n)), dma((groups, n)), dma((2, count))]
    if first:
        operands = (send, speeds, stat_in) + tables
        in_specs = [hbm, hbm, vmem] + [vmem] * 4
        out_shape += [
            jax.ShapeDtypeStruct((3, rows, m, length // m, length), jnp.bfloat16),
            jax.ShapeDtypeStruct((n, 8, 128), jnp.float32),
        ]
        scratch += [pltpu.VMEM((8, length), jnp.float32), pltpu.VMEM((8, 128), jnp.float32)]
        sems += [dma((count, m)), dma((count, m)), dma((count,)), dma((n,)), dma((n,)), dma]
    else:
        operands = (send, speeds) + tables
        in_specs = [hbm, vmem] + [vmem] * 4
    return pl.pallas_call(
        functools.partial(stage_kernel, n, m, rows, chunk, band, first),
        out_shape=out_shape,
        in_specs=in_specs,
        out_specs=[vmem] * len(out_shape),
        scratch_shapes=scratch + sems,
        compiler_params=pltpu.CompilerParams(
            collective_id=0 if first else 1,
            has_side_effects=True,
            vmem_limit_bytes=56 * 1024 * 1024,
        ),
        name="stage_one" if first else "stage_two",
    )(*operands)


def body(n, m, scalar_state, velocity, species, kappa_table, dealias_bound):
    rows = scalar_state.shape[2]
    length = scalar_state.shape[3]
    half = length // 2
    total_count = kappa_table.shape[0]
    tables = build_tables(length)
    tables = lax.optimization_barrier(tables)
    inv_y = tables[0]
    fwd_y = jnp.concatenate(
        [
            jnp.concatenate([inv_y[:length, :length], inv_y[length:, :length]], axis=1),
            jnp.concatenate([inv_y[:length, length:], inv_y[:length, :length]], axis=1),
        ],
        axis=0,
    )
    tables = tables + (fwd_y,)
    ky_index = lax.axis_index("fft") * rows + jnp.arange(rows, dtype=jnp.int32)
    ky_wave = jnp.where(ky_index < half, ky_index, ky_index - length).astype(jnp.float32)[:, None, None]
    kz_index = jnp.arange(length, dtype=jnp.int32)
    kz_wave = jnp.where(kz_index < half, kz_index, kz_index - length).astype(jnp.float32)[None, :, None]
    kx_wave = jnp.arange(half, dtype=jnp.int32).astype(jnp.float32)[None, None, :]
    ksquare = kx_wave * kx_wave + ky_wave * ky_wave + kz_wave * kz_wave
    weight = jnp.where(kx_wave == 0.0, 1.0, 2.0).astype(jnp.float32)
    cell_count = float(length) ** 3
    step_size = cfl_number * 2.0 * math.pi / length

    def z_inverse(real_part, imag_part):
        plain = jnp.concatenate([real_part, imag_part], axis=1)
        deriv = jnp.concatenate([-kz_wave * imag_part, kz_wave * real_part], axis=1)
        both = jnp.concatenate([plain, deriv], axis=2).astype(jnp.bfloat16)
        result = jnp.einsum("ab,ybx->ayx", inv_y, both, preferred_element_type=jnp.float32)
        return result.astype(jnp.bfloat16).reshape(2, n, rows, rows, 2 * half)

    def z_forward(pieces, bound):
        result = jnp.einsum(
            "rkb,byx->rykx",
            fwd_y.reshape(2, length, 2 * length),
            pieces.reshape(2 * length, rows, half),
            preferred_element_type=jnp.float32,
        )
        keep = ksquare <= bound * bound
        return jnp.where(keep, -result[0], 0.0), jnp.where(keep, -result[1], 0.0)

    start_real = scalar_state[0, 0]
    start_imag = scalar_state[0, 1]
    bound = dealias_bound[0].astype(jnp.float32)
    energy = weight * (start_real * start_real + start_imag * start_imag)
    local_var = jnp.sum(energy) / cell_count
    local_grad = jnp.sum(ksquare * energy) / cell_count
    line = jnp.arange(8, dtype=jnp.int32)[:, None]
    stat_in = jnp.broadcast_to(jnp.where(line == 0, local_var, local_grad), (8, 128))
    pieces, speeds, stats = run_stage(
        n, m, rows, True, z_inverse(start_real, start_imag), velocity, tables, stat_in
    )
    variance = jnp.sum(stats[:, 0, 0])
    mean_grad = jnp.sum(stats[:, 1, 0])
    peak_value = jnp.max(stats[:, 2, 0])
    matches = species[0] == jnp.arange(total_count, dtype=jnp.int32)
    base_kappa = jnp.sum(jnp.where(matches, kappa_table, 0.0))
    kappa = base_kappa * peak_value * jnp.sqrt(variance) / (mean_grad + 1e-06)
    factor = jnp.exp(-kappa * ksquare * step_size)
    first_real, first_imag = z_forward(pieces, bound)
    mid_real = factor * (start_real + step_size * first_real)
    mid_imag = factor * (start_imag + step_size * first_imag)
    (again,) = run_stage(n, m, rows, False, z_inverse(mid_real, mid_imag), speeds, tables)
    second_real, second_imag = z_forward(again, bound)
    new_real = factor * start_real + 0.5 * step_size * (factor * first_real + second_real)
    new_imag = factor * start_imag + 0.5 * step_size * (factor * first_imag + second_imag)
    return (jnp.stack([new_real, new_imag])[None], kappa[None])


def solution(mesh):
    placed = (
        P("scal", None, "fft", None, None),
        P(None, "fft", "scal", None),
        P("scal"),
        P(),
        P("scal"),
    )
    return jax.shard_map(
        functools.partial(body, mesh.shape["fft"], mesh.shape["scal"]),
        mesh=mesh,
        in_specs=placed,
        out_specs=(P("scal", None, "fft", None, None), P("scal")),
        check_vma=False,
    )
```

profile of v0, /device:TPU:0, one launch (start us, length us, event | category | flops | bytes accessed | tf_op | source)
XLA Modules:
  0.0 311.3 jit_solution(17160324068683359089)
XLA Ops:
  1.9 1.3 fusion.59
  3.3 0.1 broadcast_add_fusion
  3.4 1.1 fusion.70
  4.4 0.9 maximum_maximum_fusion.refs_6_.refs_5_
  5.3 0.0 copy-start.2
  5.3 2.7 bitcast_convert_fusion.1
  8.0 0.7 copy-done.2
  8.7 0.0 copy-start.7
  8.7 3.1 %fusion.57 = (f32[]{:T(128)}, f32[]{:T(128)}, bf16[16,256,128]{2,1,0:T(8,128)(2,1)}, bf16[16,256,128]{2,1,0:T(8,128)(2,1)}) fusion(f32[1,2,16,256,128]{4,3,2,1,0:T(8,128)S(1)} %copy-done.2, f32[128]{0:T(128)S(1)} %compare_select_fusion.2, f32[256]{0:T(256)S(1)} %get-tuple-element.34, f32[16,128]{1,0:T(8,128)S(1)} %broadcast_add_fusion, f32[256]{0:T(256)S(1)} %fusion.58, ...), kind=kLoop, calls=%fused_computation.74 | loop fusion | flops 6291454 | bytes 6303240 | tf_op jit(solution)/shard_map/reduce_sum | solution.py:431
  13.2 0.0 copy-done.7
  13.2 3.9 %fusion.19 = bf16[512,16,256]{2,0,1:T(8,128)(2,1)S(1)} fusion(bf16[16,256,128]{2,1,0:T(8,128)(2,1)} %get-tuple-element.27, bf16[16,256,128]{2,1,0:T(8,128)(2,1)} %get-tuple-element.28, bf16[16,256,128]{2,1,0:T(8,128)(2,1)S(1)} %get-tuple-element.30, bf16[16,256,128]{2,1,0:T(8,128)(2,1)S(1)} %get-tuple-element.29, bf16[512,512]{1,0:T(8,128)(2,1)S(1)} %copy-done.7), kind=kOutput, calls=%fused_computation.23 | convolution fusion | flops 2166358016 | bytes 8912896 | tf_op jit(solution)/shard_map/ab,ybx->ayx/dot_general | solution.py:414
  17.1 4.4 %copy.10 = bf16[512,16,256]{2,1,0:T(8,128)(2,1)} copy(bf16[512,16,256]{2,0,1:T(8,128)(2,1)S(1)} %fusion.19) | data formatting | bytes 8388608 | tf_op jit(solution)/shard_map/convert_element_type | solution.py:415
  21.5 0.7 broadcast_in_dim.49.refs_2_
  22.2 129.9 %stage_one.1 = (bf16[2,16,16,16,128]{4,3,2,1,0:T(8,128)(2,1)}, bf16[3,16,2,128,256]{4,3,2,1,0:T(8,128)(2,1)}, f32[16,8,128]{2,1,0:T(8,128)}) custom-call(bf16[2,16,16,16,256]{4,3,2,1,0:T(8,128)(2,1)} %bitcast.73, bf16[3,16,128,256]{3,2,1,0:T(8,128)(2,1)} %refs_1_.1, f32[8,128]{1,0:T(8,128)} %broadcast_in_dim.49.refs_2_, ...), custom_call_target="tpu_custom_call" | custom-call | tf_op jit(solution)/shard_map/stage_one/pallas_call | solution.py:369
  152.1 1.6 slice_reduce_fusion
  156.2 0.0 copy-start.5
  156.3 3.1 copy.11
  159.3 0.0 copy-done.5
  159.3 0.0 copy-start.3
  159.3 1.3 convolution_bitcast_fusion.1
  160.6 0.9 copy-done.3
  161.5 0.0 copy-start
  161.5 1.5 fusion.68
  163.0 0.5 copy-done
  163.6 0.3 multiply_convert_fusion.1
  163.9 0.0 copy-start.8
  163.9 0.3 multiply_convert_fusion
  164.2 0.7 copy-done.8
  164.9 2.5 fusion.16
  167.5 4.4 %copy.13 = bf16[512,16,256]{2,1,0:T(8,128)(2,1)} copy(bf16[512,16,256]{2,0,1:T(8,128)(2,1)S(1)} %fusion.16) | data formatting | bytes 8388608 | tf_op jit(solution)/shard_map/convert_element_type | solution.py:415
  171.9 127.4 %stage_two.1 = bf16[2,16,16,16,128]{4,3,2,1,0:T(8,128)(2,1)} custom-call(bf16[2,16,16,16,256]{4,3,2,1,0:T(8,128)(2,1)} %bitcast.72, bf16[3,16,2,128,256]{4,3,2,1,0:T(8,128)(2,1)} %get-tuple-element.13.refs_1_, bf16[512,512]{1,0:T(8,128)(2,1)} %constant.43.clone.refs_3_.refs_2_, bf16[256,256]{1,0:T(8,128)(2,1)} %constant.44.clone.refs_4_.refs_3_, ...), custom_call_target="tpu_custom_call" | custom-call | tf_op jit(solution)/shard_map/stage_two/pallas_call | solution.py:369
  299.3 0.0 copy-start.6
  299.3 3.1 copy.14
  302.4 0.0 copy-done.6
  302.4 0.0 copy-start.1
  302.4 0.0 copy-start.4
  302.4 1.3 convolution_bitcast_fusion
  303.7 0.9 copy-done.1
  304.6 1.3 copy-done.4
  305.9 2.0 fusion.37
  307.9 2.3 maximum_bitcast_fusion
  (6 shorter events, 0.0 us)
Async XLA Ops:
  5.3 3.4 %copy-start.2 = (f32[1,2,16,256,128]{4,3,2,1,0:T(8,128)S(1)}, f32[1,2,16,256,128]{4,3,2,1,0:T(8,128)}, u32[]{:S(2)}) copy-start(f32[1,2,16,256,128]{4,3,2,1,0:T(8,128)} %param.8) | copy-start | bytes 12582916
  8.7 4.4 %copy-start.7 = (bf16[512,512]{1,0:T(8,128)(2,1)S(1)}, bf16[512,512]{1,0:T(8,128)(2,1)}, u32[]{:S(2)}) copy-start(bf16[512,512]{1,0:T(8,128)(2,1)} %constant.43.clone.refs_3_.refs_2_) | copy-start | bytes 1572868
  156.2 3.1 copy-start.5
  159.3 2.2 copy-start.3
  161.5 2.0 copy-start
  163.9 1.0 copy-start.8
  299.3 3.1 copy-start.6
  302.4 2.2 copy-start.1
  302.4 3.5 %copy-start.4 = (f32[1,2,16,256,128]{4,3,2,1,0:T(8,128)S(1)}, f32[1,2,16,256,128]{4,3,2,1,0:T(8,128)}, u32[]{:S(2)}) copy-start(f32[1,2,16,256,128]{4,3,2,1,0:T(8,128)} %param.8) | copy-start | bytes 12582916
where the time goes:
time: 312 us; the launch traced here: 311 us
  Pallas kernels  257 us (82%)
  local copies, waits for them, and re-layouts  24.4 us (8%)
  other arithmetic  13.4 us (4%)
  matrix products  9 us (3%)
  between operations  7.13 us (2%)
    pallas_call x2, Pallas kernels, run_stage(): pl.pallas_call(functools.partial(stage_kernel, n, m, rows, chunk, band, f...  257 us
    convert_element_type x2, local copies, waits for them, and re-layouts, z_inverse(): return result.astype(jnp.bfloat16).reshape(2, n, rows, rows, 2 * half)  8.86 us
    dot_general x2, matrix products, z_inverse(): jnp.einsum('ab,ybx->ayx', inv_y, both, preferred_element_type=jnp.float32)  6.43 us

commit v1 on v0

v1 whole, which is shorter than its diff:
```python
import functools
import math

import numpy as np

import jax
import jax.numpy as jnp
from jax import lax
from jax.experimental import pallas as pl
from jax.experimental.pallas import tpu as pltpu
from jax.sharding import PartitionSpec as P

MESH = pl.DeviceIdType.MESH
cfl_number = 0.2
CHUNK = 4


def twiddle(size_in, size_out, length):
    row_index = np.arange(size_in, dtype=np.int32)[:, None]
    col_index = np.arange(size_out, dtype=np.int32)[None, :]
    angles = (row_index * col_index % length).astype(np.float32) * np.float32(2.0 * math.pi / length)
    norming = np.float32(1.0 / math.sqrt(length))
    return (np.cos(angles) * norming, np.sin(angles) * norming)


def build_tables(length, n, rows):
    half = length // 2
    quarter = half // 4
    sides = n // 2
    full_cos, full_sin = twiddle(length, length, length)
    inv_cos, inv_sin = twiddle(half, length, length)
    weight = np.where(np.arange(half) == 0, 1.0, 2.0).astype(np.float32)[:, None]
    fwd_cos, fwd_sin = twiddle(length, half, length)
    inv_z = np.block([[full_cos[:half], -full_sin[:half]], [full_sin[:half], full_cos[:half]]])
    inv_y = np.block([[full_cos, -full_sin], [full_sin, full_cos]])
    q, h, c, p, k = np.meshgrid(
        np.arange(sides), np.arange(2), np.arange(rows // CHUNK), np.arange(2), np.arange(CHUNK), indexing="ij"
    )
    inv_y = inv_y[:, ((q + h * sides) * rows + c * CHUNK + k + p * length).reshape(-1)]
    inv_x = np.concatenate([inv_cos * weight, -inv_sin * weight], axis=0)
    orders = [
        np.concatenate([((p - l - 1) % 4) * quarter + np.arange(quarter) for l in range(4)]) for p in range(4)
    ]
    fwd_x = np.stack([np.concatenate([fwd_cos[:, o], -fwd_sin[:, o]], axis=1) for o in orders])
    fwd_y = np.block([[full_cos, full_sin], [-full_sin, full_cos]])
    z, s, p = np.meshgrid(np.arange(rows), np.arange(n), np.arange(2), indexing="ij")
    fwd_z = fwd_y[:, (s * rows + z + p * length).reshape(-1)]
    return tuple(
        jnp.asarray(t.astype(np.float32).astype(jnp.bfloat16)) for t in (inv_z, inv_y, inv_x, fwd_x, fwd_y, fwd_z)
    )


def dot(a, b):
    return jnp.dot(a, b, preferred_element_type=jnp.float32)


def step_kernel(n, m, rows, band, *refs):
    (state, vel, species, ktable, bounds, inv_z, inv_y, inv_x, fwd_x, fwd_y, fwd_z,
     out, kap,
     tb, wsend, recv, tmp, uall, fsend, raw, packed, tf, zin, iny, inx, peak, acc, stat, stats,
     s_load, x_send, x_recv, w_send, w_recv, w_loc, u_send, u_recv, u_loc,
     f_send, f_recv, f_loc, t_send, t_recv, t_loc, free) = refs
    length = n * rows
    half = length // 2
    quarter = half // 4
    sides = n // 2
    nch = rows // CHUNK
    groups = rows // 4
    f32 = jnp.float32
    bf16 = jnp.bfloat16
    step_size = cfl_number * 2.0 * math.pi / length
    cells = float(length) ** 3
    me = lax.axis_index("fft")
    mine = lax.axis_index("scal")
    side = me // sides
    place = me % sides
    partner = (me + sides) % n

    def each(low, high, act):
        def one(j, carry):
            act(j)
            return carry

        lax.fori_loop(low, high, one, 0)

    def load_copy(c):
        at = pl.ds(c * CHUNK, CHUNK)
        return pltpu.make_async_copy(state.at[:, at], out.at[:, at], s_load.at[c])

    def swap_copy(c, h):
        at = pl.ds(c * CHUNK, CHUNK)
        return pltpu.make_async_remote_copy(
            src_ref=tb.at[h, at], dst_ref=tb.at[h, at], send_sem=x_send.at[c], recv_sem=x_recv.at[c],
            device_id={"fft": partner}, device_id_type=MESH,
        )

    def row_copy(st, h, c, to, slot):
        return pltpu.make_async_remote_copy(
            src_ref=wsend.at[h, c, to], dst_ref=recv.at[slot, h, c],
            send_sem=w_send.at[st, h, c, to], recv_sem=w_recv.at[st, h, c, slot],
            device_id={"fft": side * sides + to}, device_id_type=MESH,
        )

    def own_row(st, h, c):
        return pltpu.make_async_copy(wsend.at[h, c, place], recv.at[place, h, c], w_loc.at[st, h, c])

    def speed_copy(g, s, slot):
        at = pl.ds(g * 4, 4)
        return pltpu.make_async_remote_copy(
            src_ref=vel.at[:, at], dst_ref=uall.at[:, at, slot],
            send_sem=u_send.at[g, s], recv_sem=u_recv.at[g, slot],
            device_id={"scal": s}, device_id_type=MESH,
        )

    def own_speed(g):
        at = pl.ds(g * 4, 4)
        return pltpu.make_async_copy(vel.at[:, at], uall.at[:, at, mine], u_loc.at[g])

    def forward_copy(st, g, d, h, slot, k):
        return pltpu.make_async_remote_copy(
            src_ref=fsend.at[d % sides + h * sides, g, pl.ds(0, k)], dst_ref=raw.at[h, slot, g, pl.ds(0, k)],
            send_sem=f_send.at[st, g, h, d], recv_sem=f_recv.at[st, g, h, slot],
            device_id={"fft": d}, device_id_type=MESH,
        )

    def own_forward(st, g, h):
        return pltpu.make_async_copy(fsend.at[place + h * sides, g], raw.at[h, me, g], f_loc.at[st, g, h])

    def stat_copy(d, slot):
        return pltpu.make_async_remote_copy(
            src_ref=stat, dst_ref=stats.at[slot], send_sem=t_send.at[d], recv_sem=t_recv.at[slot],
            device_id={"fft": d}, device_id_type=MESH,
        )

    def needed(b, t):
        low = b * rows
        least = jnp.where(low < half, low, length - low - rows + 1)
        return (t * quarter) ** 2 + least * least <= band * band

    def by_tiles(b, act):
        for k in range(1, 4):
            wanted = needed(b, k - 1)
            if k < 3:
                wanted = jnp.logical_and(wanted, jnp.logical_not(needed(b, k)))

            @pl.when(wanted)
            def _():
                act(k)

    def chunk_inside(h, c):
        low = (place + h * sides) * rows + c * CHUNK
        least = jnp.where(low < half, low, length - low - CHUNK + 1)
        return least <= band

    each(0, nch, lambda c: load_copy(c).start())

    barrier = pltpu.get_barrier_semaphore()
    each(1, n, lambda j: pl.semaphore_signal(
        barrier, inc=1, device_id={"fft": (me + j) % n}, device_id_type=MESH))
    each(1, m, lambda j: pl.semaphore_signal(
        barrier, inc=1, device_id={"scal": (mine + j) % m}, device_id_type=MESH))

    lane = lax.broadcasted_iota(jnp.int32, (half, 2 * length), 1) % length
    flip = jnp.where((lane % 2) * side == 1, -1.0, 1.0)
    kz_lane = jnp.where(lane < half, lane, lane - length).astype(f32)
    real_z = inv_z[:half].astype(f32) * flip
    imag_z = inv_z[half:].astype(f32) * flip
    zin[0:half] = real_z.astype(bf16)
    zin[half:length] = imag_z.astype(bf16)
    zin[length:length + half] = (-kz_lane * imag_z).astype(bf16)
    zin[length + half:] = (kz_lane * real_z).astype(bf16)

    pl.semaphore_wait(barrier, n + m - 2)

    def start_speed(g):
        each(1, m, lambda j: speed_copy(g, (mine + j) % m, mine).start())
        own_speed(g).start()

    def z_pair(pr, pair):
        res = dot(zin[...], pair)
        for k in range(2):
            for f in range(2):
                for p in range(2):
                    at = f * length + p * half
                    tmp[f, pl.ds(p * CHUNK + 2 * pr + k, half, stride=2 * CHUNK), :] = (
                        res[at:at + half, k * half:(k + 1) * half]
                    )

    def send_rows(st, h, c):
        both = jnp.concatenate([tmp[0].astype(bf16), tmp[1].astype(bf16)], axis=1)
        wsend[h, c] = both.reshape(sides, rows, 2 * CHUNK, 2 * half)
        each(1, sides, lambda j: row_copy(st, h, c, (place + j) % sides, place).start())
        own_row(st, h, c).start()

    def begin(i):
        c = i % nch
        own = i < nch
        h = jnp.where(own, side, 1 - side)

        @pl.when(own)
        def _():
            load_copy(c).wait()

            def cast(r):
                tb[side, r] = out[:, r].astype(bf16)

            each(c * CHUNK, c * CHUNK + CHUNK, cast)
            swap_copy(c, side).start()

        @pl.when(jnp.logical_not(own))
        def _():
            swap_copy(c, 1 - side).wait_recv()

        def pair(pr):
            r = c * CHUNK + 2 * pr
            z_pair(pr, jnp.concatenate(
                [tb[h, r].reshape(2 * length, half), tb[h, r + 1].reshape(2 * length, half)], axis=1))

        each(0, CHUNK // 2, pair)
        send_rows(0, h, c)

    each(0, nch, begin)
    each(0, groups, start_speed)

    kx = lax.broadcasted_iota(jnp.int32, (length, half), 1).astype(f32)
    kz_row = lax.broadcasted_iota(jnp.int32, (length, half), 0)
    kz = jnp.where(kz_row < half, kz_row, kz_row - length).astype(f32)
    kxz = kx * kx + kz * kz
    weight = jnp.where(kx == 0.0, 1.0, 2.0)

    def ky_square(b, r):
        index = b * rows + r
        wave = jnp.where(index < half, index, index - length)
        return jnp.full((1, half), wave * wave, jnp.int32).astype(f32)

    acc[...] = jnp.zeros_like(acc)

    def add_row(r):
        real, imag = out[0, r], out[1, r]
        energy = weight * (real * real + imag * imag)
        acc[0] += jnp.sum(energy.reshape(length // 8, 8, half), axis=0)
        acc[1] += jnp.sum((energy * (kxz + ky_square(me, r))).reshape(length // 8, 8, half), axis=0)

    each(0, rows, add_row)

    col = lax.broadcasted_iota(jnp.int32, (length, 2 * length), 1)
    row_ky = ((col // (2 * CHUNK * nch * 2)) + ((col // (2 * CHUNK * nch)) % 2) * sides) * rows
    row_ky = row_ky + ((col // (2 * CHUNK)) % nch) * CHUNK + col % CHUNK
    row_ky = jnp.where(row_ky < half, row_ky, row_ky - length).astype(f32)
    iny[:length] = (-row_ky * inv_y[length:].astype(f32)).astype(bf16)
    iny[length:] = (row_ky * inv_y[:length].astype(f32)).astype(bf16)
    kx_row = lax.broadcasted_iota(jnp.int32, (half, length), 0).astype(f32)
    inx[:half] = (kx_row * inv_x[half:].astype(f32)).astype(bf16)
    inx[half:] = (-kx_row * inv_x[:half].astype(f32)).astype(bf16)

    for h in range(2):
        for t in range(3):
            @pl.when(jnp.logical_not(needed(place + h * sides, t)))
            def _():
                def clear(j):
                    raw[h, (me + j) % n, :, t] = jnp.zeros((groups, 2, rows, half), bf16)

                each(1, n, clear)

    peak[...] = jnp.zeros_like(peak)

    each(nch, 2 * nch, begin)

    tile_lane = lax.broadcasted_iota(jnp.int32, (2 * length, half), 1) // quarter

    def pick(choices):
        result = choices[-1]
        for i in range(len(choices) - 2, -1, -1):
            result = jnp.where(tile_lane == i, choices[i], result)
        return result

    def pair_planes(st, z, hh):
        blocks = [recv[:, :, :, z + p].reshape(2 * length, 2 * half) for p in range(2)]
        section = dot(inv_y[...], jnp.concatenate(blocks, axis=1)).astype(bf16)
        turned = dot(iny[...], jnp.concatenate([b[:, :half] for b in blocks], axis=1)).astype(bf16)
        halves = []
        for p in range(2):
            at = 2 * half * p
            sides_of = [
                (section[:, at:at + half], inx),
                (turned[:, half * p:half * (p + 1)], inv_x),
                (section[:, at + half:at + 2 * half], inv_x),
            ]
            total = None
            square = None
            for i, (part, table) in enumerate(sides_of):
                lhs = jnp.concatenate([part[:length], part[length:]], axis=1)
                grad = dot(lhs, table[...])
                u = uall[i, z + p].reshape(length, length).astype(f32)
                total = u * grad if total is None else total + u * grad
                if st == 0:
                    square = grad * grad if square is None else square + grad * grad
            if st == 0:
                peak[...] = jnp.maximum(peak[...], jnp.max(square.reshape(length // 8, 8, length), axis=0))
            flat = dot(total.astype(bf16), fwd_x[2 * hh + p]).astype(bf16)
            halves.append(jnp.concatenate([flat[:, :half], flat[:, half:]], axis=0))
        packed[hh] = dot(fwd_y[...], jnp.concatenate(halves, axis=1))

    def physical(st):
        def arrive(h):
            def chunk(c):
                each(1, sides, lambda j: row_copy(
                    st, h, c, (place + j) % sides, (place + sides - j) % sides).wait_recv())
                own_row(st, h, c).wait()

            each(0, nch, chunk)

        each(0, 2, arrive)
        if st == 0:
            def arrive_speed(g):
                each(1, m, lambda j: speed_copy(g, (mine + j) % m, (mine + m - j) % m).wait_recv())
                own_speed(g).wait()

            each(0, groups, arrive_speed)

        def run_group(g):
            for hh in range(2):
                pair_planes(st, g * 4 + 2 * hh, hh)
            for t in range(3):
                chosen = [(i + 1 + t) % 4 for i in range(4)]
                tile = pick([packed[p // 2, :, (p % 2) * half:(p % 2 + 1) * half] for p in chosen]).astype(bf16)
                for q in range(2):
                    fsend[:, g, t, q] = tile[q * length:(q + 1) * length].reshape(n, rows, half)
            if st == 1:
                @pl.when(g == 0)
                def _():
                    pl.semaphore_wait(free, n - 1)

            def leave(j):
                d = (me + j) % n
                for_blocks(st, d, lambda h: by_tiles(
                    d % sides + h * sides, lambda k: forward_copy(st, g, d, h, me, k).start()))

            each(1, n, leave)
            for_blocks(st, me, lambda h: own_forward(st, g, h).start())

        each(0, groups, run_group)

    def for_blocks(st, d, act):
        if st == 0:
            each(0, 2, act)
        else:
            act(d // sides)

    def forward_arrive(st, h):
        def group(g):
            each(1, n, lambda j: by_tiles(place + h * sides, lambda k: forward_copy(
                st, g, (me + j) % n, h, (me + n - j) % n, k).wait_recv()))
            own_forward(st, g, h).wait()

        each(0, groups, group)

    def forward_sent(st):
        def group(g):
            def one(j):
                d = (me + j) % n
                for_blocks(st, d, lambda h: by_tiles(
                    d % sides + h * sides, lambda k: forward_copy(st, g, d, h, me, k).wait_send()))

            each(1, n, one)

        each(0, groups, group)

    def rows_sent(st):
        each(0, 2, lambda h: each(0, nch, lambda c: each(
            1, sides, lambda j: row_copy(st, h, c, (place + j) % sides, place).wait_send())))

    def unpack(h):
        def group(g):
            tiles = [raw[h, :, g, t].reshape(2 * length, half).astype(f32) for t in range(3)]
            for p in range(4):
                moved = [
                    pltpu.roll(tiles[t], (2 * t + 1 - p) % 4 * quarter, 1) if (2 * t + 1 - p) % 4 else tiles[t]
                    for t in range(3)
                ]
                at = pl.multiple_of((4 * g + p) * 2 * length, 2 * length)
                tf[pl.ds(at, 2 * length), :] = pick(moved + [jnp.zeros_like(tiles[0])])

        each(0, groups, group)

    def z_forward(r):
        pair = [tf[pl.ds(r + k, 2 * length, stride=rows), :].astype(bf16) for k in range(2)]
        return dot(fwd_z[...], jnp.concatenate(pair, axis=1))

    physical(0)

    line = lax.broadcasted_iota(jnp.int32, (8, 128), 0)
    largest = jnp.sqrt(jnp.max(peak[...], keepdims=True))
    local_var = jnp.sum(acc[0], keepdims=True) / cells
    local_grad = jnp.sum(acc[1], keepdims=True) / cells
    stat[...] = jnp.where(line == 0, local_var, jnp.where(line == 1, local_grad, largest))
    each(1, n, lambda j: stat_copy((me + j) % n, me).start())
    stats[me] = stat[...]
    rows_sent(0)
    each(1, n, lambda j: stat_copy((me + j) % n, (me + n - j) % n).wait_recv())
    summed = jnp.sum(stats[...], axis=0)
    highest = jnp.max(stats[...], axis=0)
    kappa = ktable[species[0]] * highest[2:3, :1] * jnp.sqrt(summed[0:1, :1]) / (summed[1:2, :1] + 1e-06)
    kap[...] = jnp.broadcast_to(kappa, kap.shape)
    bound = jnp.full((1, half), bounds[0], jnp.int32).astype(f32)
    bound = bound * bound
    rate = -kappa * step_size

    def second(h, c, inside):
        block = place + h * sides

        def pair(pr):
            r = c * CHUNK + 2 * pr
            moved = z_forward(r) if inside else None
            cols = []
            for k in range(2):
                square = kxz + ky_square(block, r + k)
                factor = jnp.exp(rate * square)
                real = tb[h, r + k, 0].astype(f32)
                imag = tb[h, r + k, 1].astype(f32)
                if inside:
                    keep = square <= bound
                    add_real = jnp.where(keep, -step_size * moved[:length, k * half:(k + 1) * half], 0.0)
                    add_imag = jnp.where(keep, -step_size * moved[length:, k * half:(k + 1) * half], 0.0)
                    real = real + add_real
                    imag = imag + add_imag
                cols.append(jnp.concatenate([(factor * real).astype(bf16), (factor * imag).astype(bf16)], axis=0))

                @pl.when(h == side)
                def _():
                    if inside:
                        out[0, r + k] = factor * (out[0, r + k] + 0.5 * add_real)
                        out[1, r + k] = factor * (out[1, r + k] + 0.5 * add_imag)
                    else:
                        out[0, r + k] = factor * out[0, r + k]
                        out[1, r + k] = factor * out[1, r + k]

            z_pair(pr, jnp.concatenate(cols, axis=1))

        each(0, CHUNK // 2, pair)
        send_rows(1, h, c)

    def early(i):
        h, c = i // nch, i % nch

        @pl.when(jnp.logical_not(chunk_inside(h, c)))
        def _():
            second(h, c, False)

    each(0, 2 * nch, early)

    def late(i):
        h = (side + i) % 2
        forward_arrive(0, h)
        unpack(h)

        @pl.when(i == 1)
        def _():
            each(1, n, lambda j: pl.semaphore_signal(
                free, inc=1, device_id={"fft": (me + j) % n}, device_id_type=MESH))

        def chunk(c):
            @pl.when(chunk_inside(h, c))
            def _():
                second(h, c, True)

        each(0, nch, chunk)

    each(0, 2, late)
    forward_sent(0)
    physical(1)
    forward_arrive(1, side)
    unpack(side)

    def finish(c):
        @pl.when(chunk_inside(side, c))
        def _():
            def pair(pr):
                r = c * CHUNK + 2 * pr
                moved = z_forward(r)
                for k in range(2):
                    keep = kxz + ky_square(me, r + k) <= bound
                    for p in range(2):
                        value = moved[p * length:(p + 1) * length, k * half:(k + 1) * half]
                        out[p, r + k] += jnp.where(keep, -0.5 * step_size * value, 0.0)

            each(0, CHUNK // 2, pair)

    each(0, nch, finish)

    each(0, nch, lambda c: swap_copy(c, side).wait_send())
    each(0, groups, lambda g: each(1, m, lambda j: speed_copy(g, (mine + j) % m, mine).wait_send()))
    each(1, n, lambda j: stat_copy((me + j) % n, me).wait_send())
    rows_sent(1)
    forward_sent(1)


def body(n, m, scalar_state, velocity, species, kappa_table, dealias_bound):
    rows = scalar_state.shape[2]
    length = scalar_state.shape[3]
    half = length // 2
    sides = n // 2
    nch = rows // CHUNK
    groups = rows // 4
    f32, bf16 = jnp.float32, jnp.bfloat16
    tables = lax.optimization_barrier(build_tables(length, n, rows))
    vmem = pl.BlockSpec(memory_space=pltpu.VMEM)
    smem = pl.BlockSpec(memory_space=pltpu.SMEM)
    hbm = pl.BlockSpec(memory_space=pl.ANY)
    dma = pltpu.SemaphoreType.DMA
    scratch = [
        pltpu.VMEM((2, rows, 2, length, half), bf16),
        pltpu.VMEM((2, nch, sides, rows, 2 * CHUNK, 2 * half), bf16),
        pltpu.VMEM((sides, 2, nch, rows, 2 * CHUNK, 2 * half), bf16),
        pltpu.VMEM((2, half * 2 * CHUNK, half), f32),
        pltpu.VMEM((3, rows, m, length // m, length), bf16),
        pltpu.VMEM((n, groups, 3, 2, rows, half), bf16),
        pltpu.VMEM((2, n, groups, 3, 2, rows, half), bf16),
        pltpu.VMEM((2, 2 * length, 2 * half), f32),
        pltpu.VMEM((rows * 2 * length, half), f32),
        pltpu.VMEM((2 * length, 2 * length), bf16),
        pltpu.VMEM((2 * length, 2 * length), bf16),
        pltpu.VMEM((length, length), bf16),
        pltpu.VMEM((8, length), f32),
        pltpu.VMEM((2, 8, half), f32),
        pltpu.VMEM((8, 128), f32),
        pltpu.VMEM((n, 8, 128), f32),
        dma((nch,)), dma((nch,)), dma((nch,)),
        dma((2, 2, nch, sides)), dma((2, 2, nch, sides)), dma((2, 2, nch)),
        dma((groups, m)), dma((groups, m)), dma((groups,)),
        dma((2, groups, 2, n)), dma((2, groups, 2, n)), dma((2, groups, 2)),
        dma((n,)), dma((n,)), dma,
        pltpu.SemaphoreType.REGULAR,
    ]
    new_state, kappa = pl.pallas_call(
        functools.partial(step_kernel, n, m, rows, length // 3),
        out_shape=[
            jax.ShapeDtypeStruct((2, rows, length, half), f32),
            jax.ShapeDtypeStruct((8, 128), f32),
        ],
        in_specs=[hbm, hbm, smem, smem, smem] + [vmem] * 6,
        out_specs=[vmem, vmem],
        scratch_shapes=scratch,
        compiler_params=pltpu.CompilerParams(
            collective_id=0, has_side_effects=True, vmem_limit_bytes=63 * 1024 * 1024,
        ),
        name="whole_step",
    )(scalar_state[0], velocity, species, kappa_table, dealias_bound, *tables)
    return new_state[None], kappa[0, :1]


def solution(mesh):
    placed = (
        P("scal", None, "fft", None, None),
        P(None, "fft", "scal", None),
        P("scal"),
        P(),
        P("scal"),
    )
    return jax.shard_map(
        functools.partial(body, mesh.shape["fft"], mesh.shape["scal"]),
        mesh=mesh,
        in_specs=placed,
        out_specs=(P("scal", None, "fft", None, None), P("scal")),
        check_vma=False,
    )
```

time: 312 us -> 261 us (0.84)
  local copies, waits for them, and re-layouts: 24.4 us -> 5.84 us
  other arithmetic: 13.4 us -> 0 us
  matrix products: 9 us -> 0 us
  between operations: 7.13 us -> 1.93 us
  Pallas kernels: 257 us -> 253 us
    dot_general x4 -> x0, matrix products: 9 us -> none  [the longest x2 6.43 us: z_inverse(): jnp.einsum('ab,ybx->ayx', inv_y, both, preferred_element_type=jnp.float32)]
    convert_element_type x2 -> x0, local copies, waits for them, and re-layouts: 8.86 us -> none  [z_inverse(): return result.astype(jnp.bfloat16).reshape(2, n, rows, rows, 2 * half)]
    reshape x2 -> x0, local copies, waits for them, and re-layouts: 6.11 us -> none  [z_forward(): pieces.reshape(2 * length, rows, half)]
    reduce_sum x3 -> x0, other arithmetic: 6.05 us -> none  [the longest x1 3.14 us: body(): local_var = jnp.sum(energy) / cell_count]
    pallas_call x2 -> x1, Pallas kernels: 257 us -> 253 us  [body(): pl.pallas_call(functools.partial(step_kernel, n, m, rows, length // 3), o...]
where the time goes in v1:
time: 261 us
  Pallas kernels  253 us (97%)
  local copies, waits for them, and re-layouts  5.84 us (2%)
    pallas_call x1, Pallas kernels, body(): pl.pallas_call(functools.partial(step_kernel, n, m, rows, length // 3), o...  253 us

profile of v1, /device:TPU:0, one launch (start us, length us, event | category | flops | bytes accessed | tf_op | source)
XLA Modules:
  0.0 261.1 jit_solution(4581613634282461289)
XLA Ops:
  1.9 253.4 %whole_step.1 = (f32[2,16,256,128]{3,2,1,0:T(8,128)}, f32[8,128]{1,0:T(8,128)}) custom-call(f32[2,16,256,128]{3,2,1,0:T(8,128)} %bitcast.4, bf16[3,16,128,256]{3,2,1,0:T(8,128)(2,1)} %refs_1_.1, s32[1]{0:T(128)S(6)} %copy.14.refs_2_, f32[64]{0:T(128)} %refs_3_.1, s32[1]{0:T(128)S(6)} %copy.15.refs_4_, bf16[256,512]{1,0:T(8,128)(2,1)} %constant.12.clone.refs_5_, ...), custom_call_target="tpu_custom_call" | custom-call | tf_op jit(solution)/shard_map/whole_step/pallas_call | solution.py:535
  255.3 1.2 slice.3
  256.5 4.7 %copy.16 = f32[1,2,16,256,128]{4,3,2,1,0:T(8,128)} copy(f32[1,2,16,256,128]{4,3,2,1,0:T(8,128)} %bitcast.3) | data formatting | bytes 8388608

commit v2 on v1

v2 whole, which is shorter than its diff:
```python
import functools
import math

import numpy as np

import jax
import jax.numpy as jnp
from jax import lax
from jax.experimental import pallas as pl
from jax.experimental.pallas import tpu as pltpu
from jax.sharding import PartitionSpec as P

MESH = pl.DeviceIdType.MESH
cfl_number = 0.2
CHUNK = 4


def twiddle(size_in, size_out, length):
    row_index = np.arange(size_in, dtype=np.int32)[:, None]
    col_index = np.arange(size_out, dtype=np.int32)[None, :]
    angles = (row_index * col_index % length).astype(np.float32) * np.float32(2.0 * math.pi / length)
    norming = np.float32(1.0 / math.sqrt(length))
    return (np.cos(angles) * norming, np.sin(angles) * norming)


def build_tables(length, n, rows):
    half = length // 2
    quarter = half // 4
    sides = n // 2
    full_cos, full_sin = twiddle(length, length, length)
    inv_cos, inv_sin = twiddle(half, length, length)
    weight = np.where(np.arange(half) == 0, 1.0, 2.0).astype(np.float32)[:, None]
    fwd_cos, fwd_sin = twiddle(length, half, length)
    inv_z = np.block([[full_cos[:half], -full_sin[:half]], [full_sin[:half], full_cos[:half]]])
    inv_y = np.block([[full_cos, -full_sin], [full_sin, full_cos]])
    q, h, c, p, k = np.meshgrid(
        np.arange(sides), np.arange(2), np.arange(rows // CHUNK), np.arange(2), np.arange(CHUNK), indexing="ij"
    )
    inv_y = inv_y[:, ((q + h * sides) * rows + c * CHUNK + k + p * length).reshape(-1)]
    inv_x = np.concatenate([inv_cos * weight, -inv_sin * weight], axis=0)
    order = np.concatenate([(3 - l) * quarter + np.arange(quarter) for l in range(4)])
    fwd_x = np.concatenate([fwd_cos[:, order], -fwd_sin[:, order]], axis=1)
    fwd_y = np.block([[full_cos, full_sin], [-full_sin, full_cos]])
    z, s, p = np.meshgrid(np.arange(rows), np.arange(n), np.arange(2), indexing="ij")
    fwd_z = fwd_y[:, (s * rows + z + p * length).reshape(-1)]
    return tuple(
        jnp.asarray(t.astype(np.float32).astype(jnp.bfloat16)) for t in (inv_z, inv_y, inv_x, fwd_x, fwd_y, fwd_z)
    )


def dot(a, b):
    return jnp.dot(a, b, preferred_element_type=jnp.float32)


def step_kernel(n, m, rows, band, *refs):
    (state, vel, species, ktable, bounds, inv_z_in, inv_y_in, inv_x_in, fwd_x_in, fwd_y_in, fwd_z_in,
     spread, partial, kap,
     inv_z, inv_y, inv_x, base_x, fwd_y, fwd_z, fwd_x, out, lined, tb, wsend, recv, tmp, uall, fsend, raw, packed, tf, zin, iny, inx, peak, acc, stat, stats,
     s_load, tab_load, a_out, l_out, x_send, x_recv, w_send, w_recv, u_send, u_recv, u_loc,
     f_send, f_recv, t_send, t_recv, free) = refs
    length = n * rows
    half = length // 2
    quarter = half // 4
    sides = n // 2
    nch = rows // CHUNK
    groups = rows // 4
    f32 = jnp.float32
    bf16 = jnp.bfloat16
    step_size = cfl_number * 2.0 * math.pi / length
    cells = float(length) ** 3
    me = lax.axis_index("fft")
    mine = lax.axis_index("scal")
    side = me // sides
    place = me % sides
    partner = (me + sides) % n

    def each(low, high, act):
        def one(j, carry):
            act(j)
            return carry

        lax.fori_loop(low, high, one, 0)

    def load_copy(c):
        at = pl.ds(c * CHUNK, CHUNK)
        return pltpu.make_async_copy(state.at[:, at], out.at[:, at], s_load.at[c])

    def swap_copy(c, h):
        at = pl.ds(c * CHUNK, CHUNK)
        return pltpu.make_async_remote_copy(
            src_ref=tb.at[h, at], dst_ref=tb.at[h, at], send_sem=x_send, recv_sem=x_recv.at[c],
            device_id={"fft": partner}, device_id_type=MESH,
        )

    def row_copy(kind, h, c, to, slot):
        at = pl.ds(0, rows) if kind == 0 else pl.ds((kind - 1) * (rows // 2), rows // 2)
        return pltpu.make_async_remote_copy(
            src_ref=wsend.at[h, c, to, at], dst_ref=recv.at[slot, h, c, at],
            send_sem=w_send.at[kind], recv_sem=w_recv.at[kind],
            device_id={"fft": side * sides + to}, device_id_type=MESH,
        )

    def partial_copy(c):
        at = pl.ds(c * CHUNK, CHUNK)
        return pltpu.make_async_copy(out.at[:, at], partial.at[:, at], a_out)

    def spread_copy(i):
        return pltpu.make_async_copy(lined.at[i], spread.at[i], l_out)

    def speed_copy(s, slot):
        return pltpu.make_async_remote_copy(
            src_ref=vel, dst_ref=uall.at[:, :, slot], send_sem=u_send, recv_sem=u_recv,
            device_id={"scal": s}, device_id_type=MESH,
        )

    def own_speed():
        return pltpu.make_async_copy(vel, uall.at[:, :, mine], u_loc)

    def await_bytes(ref, sem):
        pltpu.make_async_copy(ref, ref, sem).wait()

    def forward_copy(st, g, d, h, slot, k):
        return pltpu.make_async_remote_copy(
            src_ref=fsend.at[d % sides + h * sides, g, pl.ds(0, k)], dst_ref=raw.at[h, slot, g, pl.ds(0, k)],
            send_sem=f_send.at[h, d], recv_sem=f_recv.at[st, g, h],
            device_id={"fft": d}, device_id_type=MESH,
        )

    def stat_copy(d, slot):
        return pltpu.make_async_remote_copy(
            src_ref=stat, dst_ref=stats.at[slot], send_sem=t_send, recv_sem=t_recv,
            device_id={"fft": d}, device_id_type=MESH,
        )

    def needed(b, t):
        low = b * rows
        least = jnp.where(low < half, low, length - low - rows + 1)
        return (t * quarter) ** 2 + least * least <= band * band

    def by_tiles(b, act):
        for k in range(1, 4):
            wanted = needed(b, k - 1)
            if k < 3:
                wanted = jnp.logical_and(wanted, jnp.logical_not(needed(b, k)))

            @pl.when(wanted)
            def _():
                act(k)

    def chunk_inside(h, c):
        low = (place + h * sides) * rows + c * CHUNK
        least = jnp.where(low < half, low, length - low - CHUNK + 1)
        return least <= band

    table_copies = [
        pltpu.make_async_copy(a, b, tab_load.at[i]) for i, (a, b) in enumerate([
            (inv_z_in, inv_z), (inv_y_in, inv_y), (inv_x_in, inv_x), (fwd_x_in, base_x), (fwd_y_in, fwd_y),
            (fwd_z_in, fwd_z)])
    ]
    table_copies[0].start()
    each(0, nch, lambda c: load_copy(c).start())
    for copy in table_copies[1:]:
        copy.start()

    barrier = pltpu.get_barrier_semaphore()
    each(1, n, lambda j: pl.semaphore_signal(
        barrier, inc=1, device_id={"fft": (me + j) % n}, device_id_type=MESH))
    each(1, m, lambda j: pl.semaphore_signal(
        barrier, inc=1, device_id={"scal": (mine + j) % m}, device_id_type=MESH))

    lane = lax.broadcasted_iota(jnp.int32, (half, 2 * length), 1) % length
    flip = jnp.where((lane % 2) * side == 1, -1.0, 1.0)
    kz_lane = jnp.where(lane < half, lane, lane - length).astype(f32)
    table_copies[0].wait()
    real_z = inv_z[:half].astype(f32) * flip
    imag_z = inv_z[half:].astype(f32) * flip
    zin[0:half] = real_z.astype(bf16)
    zin[half:length] = imag_z.astype(bf16)
    zin[length:length + half] = (-kz_lane * imag_z).astype(bf16)
    zin[length + half:] = (kz_lane * real_z).astype(bf16)

    pl.semaphore_wait(barrier, n + m - 2)

    def z_pair(pr, pair):
        res = dot(zin[...], pair)
        for k in range(2):
            for f in range(2):
                for p in range(2):
                    at = f * length + p * half
                    tmp[f, pl.ds(p * CHUNK + 2 * pr + k, half, stride=2 * CHUNK), :] = (
                        res[at:at + half, k * half:(k + 1) * half]
                    )

    def send_rows(kind, h, c):
        both = jnp.concatenate([tmp[0].astype(bf16), tmp[1].astype(bf16)], axis=1)
        wsend[h, c] = both.reshape(sides, rows, 2 * CHUNK, 2 * half)
        each(1, sides, lambda j: row_copy(kind, h, c, (place + j) % sides, place).start())
        recv[place, h, c] = wsend[h, c, place]

    def begin(i):
        c = i % nch
        own = i < nch
        h = jnp.where(own, side, 1 - side)

        @pl.when(own)
        def _():
            load_copy(c).wait()

            def cast(r):
                tb[side, r] = out[:, r].astype(bf16)

            each(c * CHUNK, c * CHUNK + CHUNK, cast)
            swap_copy(c, side).start()

        @pl.when(jnp.logical_not(own))
        def _():
            swap_copy(c, 1 - side).wait_recv()

        for pr in range(CHUNK // 2):
            r = c * CHUNK + 2 * pr
            z_pair(pr, jnp.concatenate(
                [tb[h, r].reshape(2 * length, half), tb[h, r + 1].reshape(2 * length, half)], axis=1))
        send_rows(0, h, c)

    each(0, nch, begin)
    each(1, m, lambda j: speed_copy((mine + j) % m, mine).start())
    own_speed().start()

    kx = lax.broadcasted_iota(jnp.int32, (length, half), 1).astype(f32)
    kz_row = lax.broadcasted_iota(jnp.int32, (length, half), 0)
    kz = jnp.where(kz_row < half, kz_row, kz_row - length).astype(f32)
    kxz = kx * kx + kz * kz
    weight = jnp.where(kx == 0.0, 1.0, 2.0)

    def ky_square(b, r):
        index = b * rows + r
        wave = jnp.where(index < half, index, index - length)
        return jnp.full((1, half), wave * wave, jnp.int32).astype(f32)

    acc[...] = jnp.zeros_like(acc)

    def add_row(r):
        real, imag = out[0, r], out[1, r]
        energy = weight * (real * real + imag * imag)
        acc[0] += jnp.sum(energy.reshape(length // 8, 8, half), axis=0)
        acc[1] += jnp.sum((energy * (kxz + ky_square(me, r))).reshape(length // 8, 8, half), axis=0)

    each(0, rows, add_row)

    col = lax.broadcasted_iota(jnp.int32, (length, 2 * length), 1)
    row_ky = ((col // (2 * CHUNK * nch * 2)) + ((col // (2 * CHUNK * nch)) % 2) * sides) * rows
    row_ky = row_ky + ((col // (2 * CHUNK)) % nch) * CHUNK + col % CHUNK
    row_ky = jnp.where(row_ky < half, row_ky, row_ky - length).astype(f32)
    for copy in table_copies[1:]:
        copy.wait()
    iny[:length] = (-row_ky * inv_y[length:].astype(f32)).astype(bf16)
    iny[length:] = (row_ky * inv_y[:length].astype(f32)).astype(bf16)
    for i in range(2):
        turn = base_x[:, i * half:(i + 1) * half].astype(f32)
        for p in range(4):
            fwd_x[p, :, i * half:(i + 1) * half] = (pltpu.roll(turn, p * quarter, 1) if p else turn).astype(bf16)
    kx_row = lax.broadcasted_iota(jnp.int32, (half, length), 0).astype(f32)
    inx[:half] = (kx_row * inv_x[half:].astype(f32)).astype(bf16)
    inx[half:] = (-kx_row * inv_x[:half].astype(f32)).astype(bf16)

    for h in range(2):
        for t in range(3):
            @pl.when(jnp.logical_not(needed(place + h * sides, t)))
            def _():
                def clear(j):
                    raw[h, (me + j) % n, :, t] = jnp.zeros((groups, 2, rows, half), bf16)

                each(1, n, clear)

    peak[...] = jnp.zeros_like(peak)

    each(nch, 2 * nch, begin)

    tile_lane = lax.broadcasted_iota(jnp.int32, (2 * length, half), 1) // quarter

    def pick(choices):
        result = choices[-1]
        for i in range(len(choices) - 2, -1, -1):
            result = jnp.where(tile_lane == i, choices[i], result)
        return result

    def pair_planes(st, z, hh):
        blocks = [recv[:, :, :, z + p].reshape(2 * length, 2 * half) for p in range(2)]
        section = dot(inv_y[...], jnp.concatenate(blocks, axis=1)).astype(bf16)
        turned = dot(iny[...], jnp.concatenate([b[:, :half] for b in blocks], axis=1)).astype(bf16)
        halves = []
        for p in range(2):
            at = 2 * half * p
            sides_of = [
                (section[:, at:at + half], inx),
                (turned[:, half * p:half * (p + 1)], inv_x),
                (section[:, at + half:at + 2 * half], inv_x),
            ]
            total = None
            square = None
            for i, (part, table) in enumerate(sides_of):
                lhs = jnp.concatenate([part[:length], part[length:]], axis=1)
                grad = dot(lhs, table[...])
                u = uall[i, z + p].reshape(length, length).astype(f32)
                total = u * grad if total is None else total + u * grad
                if st == 0:
                    square = grad * grad if square is None else square + grad * grad
            if st == 0:
                peak[...] = jnp.maximum(peak[...], jnp.max(square.reshape(length // 8, 8, length), axis=0))
            flat = dot(total.astype(bf16), fwd_x[2 * hh + p]).astype(bf16)
            halves.append(jnp.concatenate([flat[:, :half], flat[:, half:]], axis=0))
        packed[hh] = dot(fwd_y[...], jnp.concatenate(halves, axis=1))

    def for_blocks(st, d, act):
        if st == 0:
            each(0, 2, act)
        else:
            act(d // sides)

    def leave(st, g):
        def one(j):
            d = (me + j) % n
            for_blocks(st, d, lambda h: by_tiles(
                d % sides + h * sides, lambda k: forward_copy(st, g, d, h, me, k).start()))

        each(1, n, one)

    def rows_of(kind):
        return pl.ds(0, rows) if kind == 0 else pl.ds((kind - 1) * (rows // 2), rows // 2)

    def rows_arrive(kind):
        await_bytes(recv.at[pl.ds(0, sides - 1), :, :, rows_of(kind)], w_recv.at[kind])

    def rows_sent(kind):
        await_bytes(wsend.at[:, :, pl.ds(0, sides - 1), rows_of(kind)], w_send.at[kind])

    def run_group(st, g):
        for hh in range(2):
            pair_planes(st, g * 4 + 2 * hh, hh)
        for t in range(3):
            chosen = [(i + 1 + t) % 4 for i in range(4)]
            tile = pick([packed[p // 2, :, (p % 2) * half:(p % 2 + 1) * half] for p in chosen]).astype(bf16)
            for q in range(2):
                fsend[:, g, t, q] = tile[q * length:(q + 1) * length].reshape(n, rows, half)

    def keep_own(g, h):
        raw[h, me, g] = fsend[place + h * sides, g]

    def group_arrive(st, g, h):
        by_tiles(place + h * sides, lambda k: await_bytes(
            raw.at[h, pl.ds(0, n - 1), g, pl.ds(0, k)], f_recv.at[st, g, h]))

    def forward_sent(st):
        def one(j):
            d = (me + j) % n

            def block(h):
                b = d % sides + h * sides
                by_tiles(b, lambda k: await_bytes(fsend.at[b, :, pl.ds(0, k)], f_send.at[h, d]))

            for_blocks(st, d, block)

        each(1, n, one)

    def unpack(st, h):
        def group(g):
            group_arrive(st, g, h)
            tiles = [raw[h, :, g, t].reshape(2 * length, half).astype(f32) for t in range(3)]
            for p in range(4):
                moved = [
                    pltpu.roll(tiles[t], (2 * t + 1 - p) % 4 * quarter, 1) if (2 * t + 1 - p) % 4 else tiles[t]
                    for t in range(3)
                ]
                at = pl.multiple_of((4 * g + p) * 2 * length, 2 * length)
                tf[pl.ds(at, 2 * length), :] = pick(moved + [jnp.zeros_like(tiles[0])])

        each(0, groups, group)

    def row_pair(r):
        return jnp.concatenate(
            [tf[pl.ds(r + k, 2 * length, stride=rows), :].astype(bf16) for k in range(2)], axis=1)

    rows_arrive(0)

    await_bytes(uall.at[:, :, pl.ds(0, m - 1)], u_recv)
    own_speed().wait()

    def first_group(g):
        run_group(0, g)
        for h in range(2):
            keep_own(g, h)

        @pl.when(g == 0)
        def _():
            leave(0, g)

    each(0, groups, first_group)

    line = lax.broadcasted_iota(jnp.int32, (8, 128), 0)
    largest = jnp.sqrt(jnp.max(peak[...], keepdims=True))
    local_var = jnp.sum(acc[0], keepdims=True) / cells
    local_grad = jnp.sum(acc[1], keepdims=True) / cells
    stat[...] = jnp.where(line == 0, local_var, jnp.where(line == 1, local_grad, largest))
    each(1, n, lambda j: stat_copy((me + j) % n, me).start())
    each(1, groups, lambda g: leave(0, g))
    stats[me] = stat[...]
    rows_sent(0)
    await_bytes(stats.at[pl.ds(0, n - 1)], t_recv)
    summed = jnp.sum(stats[...], axis=0)
    highest = jnp.max(stats[...], axis=0)
    kappa = ktable[species[0]] * highest[2:3, :1] * jnp.sqrt(summed[0:1, :1]) / (summed[1:2, :1] + 1e-06)
    kap[...] = jnp.broadcast_to(kappa, kap.shape)
    bound = jnp.full((1, half), bounds[0], jnp.int32).astype(f32)
    bound = bound * bound
    rate = -kappa * step_size

    def second(h, c, own, inside):
        block = place + h * sides
        for pr in range(CHUNK // 2):
            r = c * CHUNK + 2 * pr
            moved = dot(fwd_z[...], row_pair(r)) if inside else None
            cols = []
            for k in range(2):
                square = kxz + ky_square(block, r + k)
                factor = jnp.exp(rate * square)
                keep = square <= bound
                for p in range(2):
                    value = tb[h, r + k, p].astype(f32)
                    if inside:
                        add = moved[p * length:(p + 1) * length, k * half:(k + 1) * half]
                        add = jnp.where(keep, -step_size * add, 0.0)
                        value = value + add
                    cols.append((factor * value).astype(bf16))
                    if own:
                        start = out[p, r + k]
                        out[p, r + k] = factor * (start + 0.5 * add) if inside else factor * start
            z_pair(pr, jnp.concatenate(
                [jnp.concatenate(cols[:2], axis=0), jnp.concatenate(cols[2:], axis=0)], axis=1))
        send_rows(1, h, c)
        if own:
            partial_copy(c).start()

    def chunks(own, inside):
        h = side if own else 1 - side

        def one(c):
            wanted = chunk_inside(h, c)

            @pl.when(wanted if inside else jnp.logical_not(wanted))
            def _():
                second(h, c, own, inside)

        each(0, nch, one)

    for own in (True, False):
        chunks(own, False)
    for own in (True, False):
        unpack(0, side if own else 1 - side)
        if not own:
            each(1, n, lambda j: pl.semaphore_signal(
                free, inc=1, device_id={"fft": (me + j) % n}, device_id_type=MESH))
        chunks(own, True)
    each(0, 2, lambda h: each(0, nch, lambda c: each(
        1, sides, lambda j: row_copy(2, h, c, (place + j) % sides, place).start())))

    forward_sent(0)
    for part in range(2):
        rows_arrive(1 + part)
        if part == 0:
            pl.semaphore_wait(free, n - 1)

        def last_group(g):
            run_group(1, g)
            leave(1, g)
            keep_own(g, side)

        each(part * (groups // 2), (part + 1) * (groups // 2), last_group)

    unpack(1, side)

    def line_up(i):
        lined[i] = row_pair(2 * i)
        spread_copy(i).start()

    each(0, rows // 2, line_up)

    await_bytes(tb.at[side], x_send)
    await_bytes(uall.at[:, :, pl.ds(0, m - 1)], u_send)
    await_bytes(stats.at[pl.ds(0, n - 1)], t_send)
    rows_sent(1)
    rows_sent(2)
    forward_sent(1)
    await_bytes(out, a_out)
    await_bytes(lined, l_out)


def final_kernel(rows, length, spread, partial, kap, bounds, fwd_z, out, kap_out):
    half = length // 2
    f32 = jnp.float32
    step_size = cfl_number * 2.0 * math.pi / length
    kx = lax.broadcasted_iota(jnp.int32, (length, half), 1).astype(f32)
    kz = lax.broadcasted_iota(jnp.int32, (length, half), 0)
    kz = jnp.where(kz < half, kz, kz - length).astype(f32)
    bound = jnp.full((1, half), bounds[0], jnp.int32).astype(f32)
    moved = dot(fwd_z[...], spread[0])
    for k in range(2):
        ky = lax.axis_index("fft") * rows + pl.program_id(0) * 2 + k
        ky = jnp.where(ky < half, ky, ky - length)
        square = kx * kx + kz * kz + jnp.full((1, half), ky * ky, jnp.int32).astype(f32)
        for p in range(2):
            value = moved[p * length:(p + 1) * length, k * half:(k + 1) * half]
            out[p, k] = partial[p, k] + jnp.where(square <= bound * bound, -0.5 * step_size * value, 0.0)
    kap_out[0] = kap[0, 0]


def body(n, m, scalar_state, velocity, species, kappa_table, dealias_bound):
    rows = scalar_state.shape[2]
    length = scalar_state.shape[3]
    half = length // 2
    sides = n // 2
    nch = rows // CHUNK
    groups = rows // 4
    f32, bf16 = jnp.float32, jnp.bfloat16
    tables = lax.optimization_barrier(build_tables(length, n, rows))
    vmem = pl.BlockSpec(memory_space=pltpu.VMEM)
    smem = pl.BlockSpec(memory_space=pltpu.SMEM)
    hbm = pl.BlockSpec(memory_space=pl.ANY)
    dma = pltpu.SemaphoreType.DMA
    scratch = [pltpu.VMEM(t.shape, bf16) for t in tables] + [
        pltpu.VMEM((4, length, length), bf16),
        pltpu.VMEM((2, rows, length, half), f32),
        pltpu.VMEM((rows // 2, 2 * length, 2 * half), bf16),
        pltpu.VMEM((2, rows, 2, length, half), bf16),
        pltpu.VMEM((2, nch, sides, rows, 2 * CHUNK, 2 * half), bf16),
        pltpu.VMEM((sides, 2, nch, rows, 2 * CHUNK, 2 * half), bf16),
        pltpu.VMEM((2, half * 2 * CHUNK, half), f32),
        pltpu.VMEM((3, rows, m, length // m, length), bf16),
        pltpu.VMEM((n, groups, 3, 2, rows, half), bf16),
        pltpu.VMEM((2, n, groups, 3, 2, rows, half), bf16),
        pltpu.VMEM((2, 2 * length, 2 * half), f32),
        pltpu.VMEM((rows * 2 * length, half), f32),
        pltpu.VMEM((2 * length, 2 * length), bf16),
        pltpu.VMEM((2 * length, 2 * length), bf16),
        pltpu.VMEM((length, length), bf16),
        pltpu.VMEM((8, length), f32),
        pltpu.VMEM((2, 8, half), f32),
        pltpu.VMEM((8, 128), f32),
        pltpu.VMEM((n, 8, 128), f32),
        dma((nch,)), dma((len(tables),)), dma, dma, dma, dma((nch,)), dma((3,)), dma((3,)), dma, dma, dma,
        dma((2, n)), dma((2, groups, 2)), dma, dma,
        pltpu.SemaphoreType.REGULAR,
    ]
    spread, partial, kappa = pl.pallas_call(
        functools.partial(step_kernel, n, m, rows, length // 3),
        out_shape=[
            jax.ShapeDtypeStruct((rows // 2, 2 * length, 2 * half), bf16),
            jax.ShapeDtypeStruct((2, rows, length, half), f32),
            jax.ShapeDtypeStruct((8, 128), f32),
        ],
        in_specs=[hbm, hbm, smem, smem, smem] + [hbm] * 6,
        out_specs=[hbm, hbm, vmem],
        scratch_shapes=scratch,
        compiler_params=pltpu.CompilerParams(
            collective_id=0, has_side_effects=True, vmem_limit_bytes=63 * 1024 * 1024,
        ),
        name="whole_step",
    )(scalar_state[0], velocity, species, kappa_table, dealias_bound, *tables)
    new_state, kappa = pl.pallas_call(
        functools.partial(final_kernel, rows, length),
        grid=(rows // 2,),
        out_shape=[
            jax.ShapeDtypeStruct((2, rows, length, half), f32),
            jax.ShapeDtypeStruct((1,), f32),
        ],
        in_specs=[
            pl.BlockSpec((1, 2 * length, 2 * half), lambda i: (i, 0, 0)),
            pl.BlockSpec((2, 2, length, half), lambda i: (0, i, 0, 0)),
            smem, smem, vmem,
        ],
        out_specs=[pl.BlockSpec((2, 2, length, half), lambda i: (0, i, 0, 0)), smem],
        name="final_step",
    )(spread, partial, kappa, dealias_bound, tables[5])
    return new_state[None], kappa


def solution(mesh):
    placed = (
        P("scal", None, "fft", None, None),
        P(None, "fft", "scal", None),
        P("scal"),
        P(),
        P("scal"),
    )
    return jax.shard_map(
        functools.partial(body, mesh.shape["fft"], mesh.shape["scal"]),
        mesh=mesh,
        in_specs=placed,
        out_specs=(P("scal", None, "fft", None, None), P("scal")),
        check_vma=False,
    )
```

time: 261 us -> 240 us (0.920)
  Pallas kernels: 253 us -> 238 us
  local copies, waits for them, and re-layouts: 5.84 us -> 0 us
    pallas_call x1, Pallas kernels: 253 us -> 230 us  [body(): pl.pallas_call(functools.partial(step_kernel, n, m, rows, length // 3), o...]
    pallas_call x0 -> x1, Pallas kernels: none -> 8.19 us  [body(): pl.pallas_call(functools.partial(final_kernel, rows, length), grid=(rows...]
    unnamed x1 -> x0, local copies, waits for them, and re-layouts: 4.65 us -> none
where the time goes in v2:
time: 240 us
  Pallas kernels  238 us (99%)
    pallas_call x1, Pallas kernels, body(): pl.pallas_call(functools.partial(step_kernel, n, m, rows, length // 3), o...  230 us
    pallas_call x1, Pallas kernels, body(): pl.pallas_call(functools.partial(final_kernel, rows, length), grid=(rows...  8.19 us

profile of v2, /device:TPU:0, one launch (start us, length us, event | category | flops | bytes accessed | tf_op | source)
XLA Modules:
  0.0 239.7 jit_solution(10805605757198965975)
XLA Ops:
  1.9 229.6 %whole_step.1 = (bf16[8,512,256]{2,1,0:T(8,128)(2,1)}, f32[2,16,256,128]{3,2,1,0:T(8,128)}, f32[8,128]{1,0:T(8,128)}) custom-call(f32[2,16,256,128]{3,2,1,0:T(8,128)} %bitcast.2, bf16[3,16,128,256]{3,2,1,0:T(8,128)(2,1)} %refs_1_.1, s32[1]{0:T(128)S(6)} %copy.13.refs_2_, f32[64]{0:T(128)} %refs_3_.1, s32[1]{0:T(128)S(6)} %copy.14.refs_4_.bounds, ...), custom_call_target="tpu_custom_call" | custom-call | tf_op jit(solution)/shard_map/whole_step/pallas_call | solution.py:553
  231.6 8.2 %final_step.1 = (f32[2,16,256,128]{3,2,1,0:T(8,128)}, f32[1]{0:T(128)}) custom-call(bf16[8,512,256]{2,1,0:T(8,128)(2,1)} %get-tuple-element.19.spread, f32[2,16,256,128]{3,2,1,0:T(8,128)} %get-tuple-element.20.partial, f32[8,128]{1,0:T(8,128)} %get-tuple-element.21.kap, s32[1]{0:T(128)S(6)} %copy.14.refs_4_.bounds, ...), custom_call_target="tpu_custom_call" | custom-call | tf_op jit(solution)/shard_map/final_step/pallas_call | solution.py:568

commit v3 on v2

--- a/solution.py
+++ b/solution.py
@@ -317,11 +317,12 @@
         else:
             act(d // sides)
 
-    def leave(st, g):
+    def leave(st, low, high, own):
         def one(j):
             d = (me + j) % n
-            for_blocks(st, d, lambda h: by_tiles(
-                d % sides + h * sides, lambda k: forward_copy(st, g, d, h, me, k).start()))
+            h = d // sides if own else 1 - d // sides
+            by_tiles(d % sides + h * sides, lambda k: each(
+                low, high, lambda g: forward_copy(st, g, d, h, me, k).start()))
 
         each(1, n, one)
 
@@ -390,9 +391,9 @@
         for h in range(2):
             keep_own(g, h)
 
-        @pl.when(g == 0)
+        @pl.when(g < 2)
         def _():
-            leave(0, g)
+            leave(0, g, g + 1, True)
 
     each(0, groups, first_group)
 
@@ -402,7 +403,8 @@
     local_grad = jnp.sum(acc[1], keepdims=True) / cells
     stat[...] = jnp.where(line == 0, local_var, jnp.where(line == 1, local_grad, largest))
     each(1, n, lambda j: stat_copy((me + j) % n, me).start())
-    each(1, groups, lambda g: leave(0, g))
+    leave(0, 2, groups, True)
+    leave(0, 0, groups, False)
     stats[me] = stat[...]
     rows_sent(0)
     await_bytes(stats.at[pl.ds(0, n - 1)], t_recv)
@@ -413,6 +415,9 @@
     bound = jnp.full((1, half), bounds[0], jnp.int32).astype(f32)
     bound = bound * bound
     rate = -kappa * step_size
+
+    def send_upper(h, c):
+        each(1, sides, lambda j: row_copy(2, h, c, (place + j) % sides, place).start())
 
     def second(h, c, own, inside):
         block = place + h * sides
@@ -437,6 +442,8 @@
             z_pair(pr, jnp.concatenate(
                 [jnp.concatenate(cols[:2], axis=0), jnp.concatenate(cols[2:], axis=0)], axis=1))
         send_rows(1, h, c)
+        if not inside:
+            send_upper(h, c)
         if own:
             partial_copy(c).start()
 
@@ -460,8 +467,15 @@
             each(1, n, lambda j: pl.semaphore_signal(
                 free, inc=1, device_id={"fft": (me + j) % n}, device_id_type=MESH))
         chunks(own, True)
-    each(0, 2, lambda h: each(0, nch, lambda c: each(
-        1, sides, lambda j: row_copy(2, h, c, (place + j) % sides, place).start())))
+
+    def upper(i):
+        h, c = i // nch, i % nch
+
+        @pl.when(chunk_inside(h, c))
+        def _():
+            send_upper(h, c)
+
+    each(0, 2 * nch, upper)
 
     forward_sent(0)
     for part in range(2):
@@ -471,7 +485,7 @@
 
         def last_group(g):
             run_group(1, g)
-            leave(1, g)
+            leave(1, g, g + 1, True)
             keep_own(g, side)
 
         each(part * (groups // 2), (part + 1) * (groups // 2), last_group)
@@ -494,23 +508,62 @@
     await_bytes(lined, l_out)
 
 
-def final_kernel(rows, length, spread, partial, kap, bounds, fwd_z, out, kap_out):
+def final_kernel(rows, length, spread, partial, kap, bounds, fwd_z_in, out, kap_out, fwd_z, lined, base, done,
+                 t_load, l_load, b_load, d_out):
     half = length // 2
     f32 = jnp.float32
     step_size = cfl_number * 2.0 * math.pi / length
+    pairs = rows // 2
+
+    def each(act):
+        def one(i, carry):
+            act(i)
+            return carry
+
+        lax.fori_loop(0, pairs, one, 0)
+
+    def line_copy(i):
+        return pltpu.make_async_copy(spread.at[i], lined.at[i], l_load.at[i])
+
+    def base_copy(i):
+        at = pl.ds(2 * i, 2)
+        return pltpu.make_async_copy(partial.at[:, at], base.at[:, at], b_load.at[i])
+
+    def done_copy(i):
+        at = pl.ds(2 * i, 2)
+        return pltpu.make_async_copy(done.at[:, at], out.at[:, at], d_out.at[i])
+
+    table = pltpu.make_async_copy(fwd_z_in, fwd_z, t_load)
+    table.start()
+
+    def load(i):
+        line_copy(i).start()
+        base_copy(i).start()
+
+    each(load)
     kx = lax.broadcasted_iota(jnp.int32, (length, half), 1).astype(f32)
     kz = lax.broadcasted_iota(jnp.int32, (length, half), 0)
     kz = jnp.where(kz < half, kz, kz - length).astype(f32)
     bound = jnp.full((1, half), bounds[0], jnp.int32).astype(f32)
-    moved = dot(fwd_z[...], spread[0])
-    for k in range(2):
-        ky = lax.axis_index("fft") * rows + pl.program_id(0) * 2 + k
-        ky = jnp.where(ky < half, ky, ky - length)
-        square = kx * kx + kz * kz + jnp.full((1, half), ky * ky, jnp.int32).astype(f32)
-        for p in range(2):
-            value = moved[p * length:(p + 1) * length, k * half:(k + 1) * half]
-            out[p, k] = partial[p, k] + jnp.where(square <= bound * bound, -0.5 * step_size * value, 0.0)
+    kxz = kx * kx + kz * kz
     kap_out[0] = kap[0, 0]
+    table.wait()
+
+    def pair(i):
+        line_copy(i).wait()
+        base_copy(i).wait()
+        moved = dot(fwd_z[...], lined[i])
+        for k in range(2):
+            ky = lax.axis_index("fft") * rows + i * 2 + k
+            ky = jnp.where(ky < half, ky, ky - length)
+            keep = kxz + jnp.full((1, half), ky * ky, jnp.int32).astype(f32) <= bound * bound
+            for p in range(2):
+                value = moved[p * length:(p + 1) * length, k * half:(k + 1) * half]
+                done[p, 2 * i + k] = base[p, 2 * i + k] + jnp.where(keep, -0.5 * step_size * value, 0.0)
+        done_copy(i).start()
+
+    each(pair)
+    each(lambda i: done_copy(i).wait())
 
 
 def body(n, m, scalar_state, velocity, species, kappa_table, dealias_bound):
@@ -567,17 +620,19 @@
     )(scalar_state[0], velocity, species, kappa_table, dealias_bound, *tables)
     new_state, kappa = pl.pallas_call(
         functools.partial(final_kernel, rows, length),
-        grid=(rows // 2,),
         out_shape=[
             jax.ShapeDtypeStruct((2, rows, length, half), f32),
             jax.ShapeDtypeStruct((1,), f32),
         ],
-        in_specs=[
-            pl.BlockSpec((1, 2 * length, 2 * half), lambda i: (i, 0, 0)),
-            pl.BlockSpec((2, 2, length, half), lambda i: (0, i, 0, 0)),
-            smem, smem, vmem,
+        in_specs=[hbm, hbm, smem, smem, hbm],
+        out_specs=[hbm, smem],
+        scratch_shapes=[
+            pltpu.VMEM((2 * length, 2 * length), bf16),
+            pltpu.VMEM((rows // 2, 2 * length, 2 * half), bf16),
+            pltpu.VMEM((2, rows, length, half), f32),
+            pltpu.VMEM((2, rows, length, half), f32),
+            dma, dma((rows // 2,)), dma((rows // 2,)), dma((rows // 2,)),
         ],
-        out_specs=[pl.BlockSpec((2, 2, length, half), lambda i: (0, i, 0, 0)), smem],
         name="final_step",
     )(spread, partial, kappa, dealias_bound, tables[5])
     return new_state[None], kappa

time: 240 us -> 230 us (0.958)
  Pallas kernels: 238 us -> 228 us
    pallas_call x1, Pallas kernels: 230 us -> 221 us  [body(): pl.pallas_call(functools.partial(step_kernel, n, m, rows, length // 3), o...]
where the time goes in v3:
time: 230 us
  Pallas kernels  228 us (99%)
    pallas_call x1, Pallas kernels, body(): pl.pallas_call(functools.partial(step_kernel, n, m, rows, length // 3), o...  221 us
    pallas_call x1, Pallas kernels, body(): pl.pallas_call(functools.partial(final_kernel, rows, length), out_shape=[...  6.25 us

profile of v3, /device:TPU:0, one launch (start us, length us, event | category | flops | bytes accessed | tf_op | source)
XLA Modules:
  0.0 229.8 jit_solution(14850487734784614454)
XLA Ops:
  1.9 221.5 %whole_step.1 = (bf16[8,512,256]{2,1,0:T(8,128)(2,1)}, f32[2,16,256,128]{3,2,1,0:T(8,128)}, f32[8,128]{1,0:T(8,128)}) custom-call(f32[2,16,256,128]{3,2,1,0:T(8,128)} %bitcast.2, bf16[3,16,128,256]{3,2,1,0:T(8,128)(2,1)} %refs_1_.1, s32[1]{0:T(128)S(6)} %copy.13.refs_2_, f32[64]{0:T(128)} %refs_3_.1, s32[1]{0:T(128)S(6)} %copy.14.refs_4_.bounds, ...), custom_call_target="tpu_custom_call" | custom-call | tf_op jit(solution)/shard_map/whole_step/pallas_call | solution.py:606
  223.4 6.2 %final_step.1 = (f32[2,16,256,128]{3,2,1,0:T(8,128)}, f32[1]{0:T(128)}) custom-call(bf16[8,512,256]{2,1,0:T(8,128)(2,1)} %get-tuple-element.19.spread, f32[2,16,256,128]{3,2,1,0:T(8,128)} %get-tuple-element.20.partial, f32[8,128]{1,0:T(8,128)} %get-tuple-element.21.kap, s32[1]{0:T(128)S(6)} %copy.14.refs_4_.bounds, ...), custom_call_target="tpu_custom_call" | custom-call | tf_op jit(solution)/shard_map/final_step/pallas_call | solution.py:621

commit v4 on v3

--- a/solution.py
+++ b/solution.py
@@ -54,9 +54,9 @@
 
 def step_kernel(n, m, rows, band, *refs):
     (state, vel, species, ktable, bounds, inv_z_in, inv_y_in, inv_x_in, fwd_x_in, fwd_y_in, fwd_z_in,
-     spread, partial, kap,
-     inv_z, inv_y, inv_x, base_x, fwd_y, fwd_z, fwd_x, out, lined, tb, wsend, recv, tmp, uall, fsend, raw, packed, tf, zin, iny, inx, peak, acc, stat, stats,
-     s_load, tab_load, a_out, l_out, x_send, x_recv, w_send, w_recv, u_send, u_recv, u_loc,
+     out, lined, kap,
+     inv_z, inv_y, inv_x, base_x, fwd_y, fwd_z, fwd_x, tb, wsend, recv, tmp, uall, fsend, raw, packed, tf, zin, iny, inx, peak, acc, stat, stats,
+     s_load, tab_load, x_send, x_recv, w_send, w_recv, u_send, u_recv, u_loc,
      f_send, f_recv, t_send, t_recv, free) = refs
     length = n * rows
     half = length // 2
@@ -92,20 +92,32 @@
             device_id={"fft": partner}, device_id_type=MESH,
         )
 
+    lower = groups // 2
+
+    def planes_of(kind):
+        if isinstance(kind, int) and kind in (0, 2):
+            return pl.ds(0, lower * 4)
+        if isinstance(kind, int) and kind == 1:
+            return pl.ds(lower * 4, (groups - lower) * 4)
+        return pl.ds((lower + kind - 3) * 4, 4)
+
+    uppers = range(3, 3 + groups - lower)
+
     def row_copy(kind, h, c, to, slot):
-        at = pl.ds(0, rows) if kind == 0 else pl.ds((kind - 1) * (rows // 2), rows // 2)
+        at = planes_of(kind)
         return pltpu.make_async_remote_copy(
             src_ref=wsend.at[h, c, to, at], dst_ref=recv.at[slot, h, c, at],
             send_sem=w_send.at[kind], recv_sem=w_recv.at[kind],
             device_id={"fft": side * sides + to}, device_id_type=MESH,
         )
 
-    def partial_copy(c):
-        at = pl.ds(c * CHUNK, CHUNK)
-        return pltpu.make_async_copy(out.at[:, at], partial.at[:, at], a_out)
-
-    def spread_copy(i):
-        return pltpu.make_async_copy(lined.at[i], spread.at[i], l_out)
+    def block_copy(kind, h, to, slot):
+        at = planes_of(kind)
+        return pltpu.make_async_remote_copy(
+            src_ref=wsend.at[h, :, to, at], dst_ref=recv.at[slot, h, :, at],
+            send_sem=w_send.at[kind], recv_sem=w_recv.at[kind],
+            device_id={"fft": side * sides + to}, device_id_type=MESH,
+        )
 
     def speed_copy(s, slot):
         return pltpu.make_async_remote_copy(
@@ -147,9 +159,9 @@
             def _():
                 act(k)
 
-    def chunk_inside(h, c):
-        low = (place + h * sides) * rows + c * CHUNK
-        least = jnp.where(low < half, low, length - low - CHUNK + 1)
+    def block_inside(h):
+        low = (place + h * sides) * rows
+        least = jnp.where(low < half, low, length - low - rows + 1)
         return least <= band
 
     table_copies = [
@@ -191,10 +203,11 @@
                         res[at:at + half, k * half:(k + 1) * half]
                     )
 
-    def send_rows(kind, h, c):
+    def send_rows(kinds, h, c):
         both = jnp.concatenate([tmp[0].astype(bf16), tmp[1].astype(bf16)], axis=1)
         wsend[h, c] = both.reshape(sides, rows, 2 * CHUNK, 2 * half)
-        each(1, sides, lambda j: row_copy(kind, h, c, (place + j) % sides, place).start())
+        for kind in kinds:
+            each(1, sides, lambda j: row_copy(kind, h, c, (place + j) % sides, place).start())
         recv[place, h, c] = wsend[h, c, place]
 
     def begin(i):
@@ -220,7 +233,7 @@
             r = c * CHUNK + 2 * pr
             z_pair(pr, jnp.concatenate(
                 [tb[h, r].reshape(2 * length, half), tb[h, r + 1].reshape(2 * length, half)], axis=1))
-        send_rows(0, h, c)
+        send_rows((0, 1), h, c)
 
     each(0, nch, begin)
     each(1, m, lambda j: speed_copy((mine + j) % m, mine).start())
@@ -284,10 +297,13 @@
             result = jnp.where(tile_lane == i, choices[i], result)
         return result
 
-    def pair_planes(st, z, hh):
+    def planes_in(z):
         blocks = [recv[:, :, :, z + p].reshape(2 * length, 2 * half) for p in range(2)]
         section = dot(inv_y[...], jnp.concatenate(blocks, axis=1)).astype(bf16)
         turned = dot(iny[...], jnp.concatenate([b[:, :half] for b in blocks], axis=1)).astype(bf16)
+        return section, turned
+
+    def planes_out(st, z, hh, section, turned):
         halves = []
         for p in range(2):
             at = 2 * half * p
@@ -309,7 +325,7 @@
                 peak[...] = jnp.maximum(peak[...], jnp.max(square.reshape(length // 8, 8, length), axis=0))
             flat = dot(total.astype(bf16), fwd_x[2 * hh + p]).astype(bf16)
             halves.append(jnp.concatenate([flat[:, :half], flat[:, half:]], axis=0))
-        packed[hh] = dot(fwd_y[...], jnp.concatenate(halves, axis=1))
+        return jnp.concatenate(halves, axis=1)
 
     def for_blocks(st, d, act):
         if st == 0:
@@ -317,27 +333,33 @@
         else:
             act(d // sides)
 
-    def leave(st, low, high, own):
+    def leave(st, low, high, own, across=None):
         def one(j):
-            d = (me + j) % n
-            h = d // sides if own else 1 - d // sides
-            by_tiles(d % sides + h * sides, lambda k: each(
-                low, high, lambda g: forward_copy(st, g, d, h, me, k).start()))
+            d = (me + jnp.where(side == st, j, n - j)) % n
+
+            def send():
+                h = d // sides if own else 1 - d // sides
+                by_tiles(d % sides + h * sides, lambda k: each(
+                    low, high, lambda g: forward_copy(st, g, d, h, me, k).start()))
+
+            if across is None:
+                send()
+            else:
+                pl.when((d // sides != side) if across else (d // sides == side))(send)
 
         each(1, n, one)
 
-    def rows_of(kind):
-        return pl.ds(0, rows) if kind == 0 else pl.ds((kind - 1) * (rows // 2), rows // 2)
-
     def rows_arrive(kind):
-        await_bytes(recv.at[pl.ds(0, sides - 1), :, :, rows_of(kind)], w_recv.at[kind])
+        await_bytes(recv.at[pl.ds(0, sides - 1), :, :, planes_of(kind)], w_recv.at[kind])
 
     def rows_sent(kind):
-        await_bytes(wsend.at[:, :, pl.ds(0, sides - 1), rows_of(kind)], w_send.at[kind])
+        await_bytes(wsend.at[:, :, pl.ds(0, sides - 1), planes_of(kind)], w_send.at[kind])
 
     def run_group(st, g):
+        inner = [planes_in(g * 4 + 2 * hh) for hh in range(2)]
+        lines = [planes_out(st, g * 4 + 2 * hh, hh, *inner[hh]) for hh in range(2)]
         for hh in range(2):
-            pair_planes(st, g * 4 + 2 * hh, hh)
+            packed[hh] = dot(fwd_y[...], lines[hh])
         for t in range(3):
             chosen = [(i + 1 + t) % 4 for i in range(4)]
             tile = pick([packed[p // 2, :, (p % 2) * half:(p % 2 + 1) * half] for p in chosen]).astype(bf16)
@@ -362,6 +384,10 @@
             for_blocks(st, d, block)
 
         each(1, n, one)
+
+    def row_pair(r, base, size):
+        return jnp.concatenate(
+            [tf[pl.ds(base + r + k, size, stride=rows), :].astype(bf16) for k in range(2)], axis=1)
 
     def unpack(st, h):
         def group(g):
@@ -374,19 +400,25 @@
                 ]
                 at = pl.multiple_of((4 * g + p) * 2 * length, 2 * length)
                 tf[pl.ds(at, 2 * length), :] = pick(moved + [jnp.zeros_like(tiles[0])])
+            if st == 1:
+                size = 2 * length // groups
+                for i in range(rows // 2):
+                    lined[i, pl.ds(pl.multiple_of(g * size, size), size)] = row_pair(2 * i, g * 8 * length, size)
 
         each(0, groups, group)
-
-    def row_pair(r):
-        return jnp.concatenate(
-            [tf[pl.ds(r + k, 2 * length, stride=rows), :].astype(bf16) for k in range(2)], axis=1)
-
-    rows_arrive(0)
 
     await_bytes(uall.at[:, :, pl.ds(0, m - 1)], u_recv)
     own_speed().wait()
 
     def first_group(g):
+        @pl.when(g == 0)
+        def _():
+            rows_arrive(0)
+
+        @pl.when(g == lower)
+        def _():
+            rows_arrive(1)
+
         run_group(0, g)
         for h in range(2):
             keep_own(g, h)
@@ -403,11 +435,23 @@
     local_grad = jnp.sum(acc[1], keepdims=True) / cells
     stat[...] = jnp.where(line == 0, local_var, jnp.where(line == 1, local_grad, largest))
     each(1, n, lambda j: stat_copy((me + j) % n, me).start())
-    leave(0, 2, groups, True)
-    leave(0, 0, groups, False)
+    leave(0, 2, min(3, groups), True)
+    outer = (place < sides // 2) == (side == 0)
+
+    @pl.when(outer)
+    def _():
+        leave(0, min(3, groups), groups, True)
+        leave(0, 0, groups, False)
+
     stats[me] = stat[...]
     rows_sent(0)
+    rows_sent(1)
     await_bytes(stats.at[pl.ds(0, n - 1)], t_recv)
+    @pl.when(jnp.logical_not(outer))
+    def _():
+        leave(0, min(3, groups), groups, True)
+        leave(0, 0, groups, False, False)
+
     summed = jnp.sum(stats[...], axis=0)
     highest = jnp.max(stats[...], axis=0)
     kappa = ktable[species[0]] * highest[2:3, :1] * jnp.sqrt(summed[0:1, :1]) / (summed[1:2, :1] + 1e-06)
@@ -416,14 +460,15 @@
     bound = bound * bound
     rate = -kappa * step_size
 
-    def send_upper(h, c):
-        each(1, sides, lambda j: row_copy(2, h, c, (place + j) % sides, place).start())
+    def send_upper(h):
+        for kind in uppers:
+            each(1, sides, lambda j: block_copy(kind, h, (place + j) % sides, place).start())
 
     def second(h, c, own, inside):
         block = place + h * sides
         for pr in range(CHUNK // 2):
             r = c * CHUNK + 2 * pr
-            moved = dot(fwd_z[...], row_pair(r)) if inside else None
+            moved = dot(fwd_z[...], row_pair(r, 0, 2 * length)) if inside else None
             cols = []
             for k in range(2):
                 square = kxz + ky_square(block, r + k)
@@ -441,75 +486,63 @@
                         out[p, r + k] = factor * (start + 0.5 * add) if inside else factor * start
             z_pair(pr, jnp.concatenate(
                 [jnp.concatenate(cols[:2], axis=0), jnp.concatenate(cols[2:], axis=0)], axis=1))
-        send_rows(1, h, c)
-        if not inside:
-            send_upper(h, c)
-        if own:
-            partial_copy(c).start()
+        send_rows((2,), h, c)
 
     def chunks(own, inside):
         h = side if own else 1 - side
-
-        def one(c):
-            wanted = chunk_inside(h, c)
-
-            @pl.when(wanted if inside else jnp.logical_not(wanted))
-            def _():
-                second(h, c, own, inside)
-
-        each(0, nch, one)
+        wanted = block_inside(h)
+
+        @pl.when(wanted if inside else jnp.logical_not(wanted))
+        def _():
+            each(0, nch, lambda c: second(h, c, own, inside))
+            if not inside:
+                send_upper(h)
 
     for own in (True, False):
         chunks(own, False)
     for own in (True, False):
         unpack(0, side if own else 1 - side)
-        if not own:
+        if own:
+            @pl.when(jnp.logical_not(outer))
+            def _():
+                leave(0, 0, groups, False, True)
+        else:
             each(1, n, lambda j: pl.semaphore_signal(
                 free, inc=1, device_id={"fft": (me + j) % n}, device_id_type=MESH))
         chunks(own, True)
 
-    def upper(i):
-        h, c = i // nch, i % nch
-
-        @pl.when(chunk_inside(h, c))
-        def _():
-            send_upper(h, c)
-
-    each(0, 2 * nch, upper)
+    for h in range(2):
+        @pl.when(block_inside(h))
+        def _():
+            send_upper(h)
 
     forward_sent(0)
-    for part in range(2):
-        rows_arrive(1 + part)
-        if part == 0:
+
+    def last_group(g):
+        @pl.when(g == 0)
+        def _():
+            rows_arrive(2)
             pl.semaphore_wait(free, n - 1)
 
-        def last_group(g):
-            run_group(1, g)
-            leave(1, g, g + 1, True)
-            keep_own(g, side)
-
-        each(part * (groups // 2), (part + 1) * (groups // 2), last_group)
-
-    unpack(1, side)
-
-    def line_up(i):
-        lined[i] = row_pair(2 * i)
-        spread_copy(i).start()
-
-    each(0, rows // 2, line_up)
-
+        @pl.when(g >= lower)
+        def _():
+            rows_arrive(3 + g - lower)
+
+        run_group(1, g)
+        leave(1, g, g + 1, True)
+        keep_own(g, side)
+
+    each(0, groups, last_group)
     await_bytes(tb.at[side], x_send)
     await_bytes(uall.at[:, :, pl.ds(0, m - 1)], u_send)
     await_bytes(stats.at[pl.ds(0, n - 1)], t_send)
-    rows_sent(1)
-    rows_sent(2)
+    for kind in (2, *uppers):
+        rows_sent(kind)
+    unpack(1, side)
     forward_sent(1)
-    await_bytes(out, a_out)
-    await_bytes(lined, l_out)
-
-
-def final_kernel(rows, length, spread, partial, kap, bounds, fwd_z_in, out, kap_out, fwd_z, lined, base, done,
-                 t_load, l_load, b_load, d_out):
+
+
+def final_kernel(rows, length, partial, lined, kap, bounds, fwd_z_in, out, kap_out, fwd_z, done, t_load, d_out):
     half = length // 2
     f32 = jnp.float32
     step_size = cfl_number * 2.0 * math.pi / length
@@ -520,14 +553,7 @@
             act(i)
             return carry
 
-        lax.fori_loop(0, pairs, one, 0)
-
-    def line_copy(i):
-        return pltpu.make_async_copy(spread.at[i], lined.at[i], l_load.at[i])
-
-    def base_copy(i):
-        at = pl.ds(2 * i, 2)
-        return pltpu.make_async_copy(partial.at[:, at], base.at[:, at], b_load.at[i])
+        lax.fori_loop(0, pairs, one, 0, unroll=2)
 
     def done_copy(i):
         at = pl.ds(2 * i, 2)
@@ -536,22 +562,15 @@
     table = pltpu.make_async_copy(fwd_z_in, fwd_z, t_load)
     table.start()
 
-    def load(i):
-        line_copy(i).start()
-        base_copy(i).start()
-
-    each(load)
     kx = lax.broadcasted_iota(jnp.int32, (length, half), 1).astype(f32)
     kz = lax.broadcasted_iota(jnp.int32, (length, half), 0)
     kz = jnp.where(kz < half, kz, kz - length).astype(f32)
     bound = jnp.full((1, half), bounds[0], jnp.int32).astype(f32)
     kxz = kx * kx + kz * kz
-    kap_out[0] = kap[0, 0]
+    kap_out[0] = jnp.max(kap[...])
     table.wait()
 
     def pair(i):
-        line_copy(i).wait()
-        base_copy(i).wait()
         moved = dot(fwd_z[...], lined[i])
         for k in range(2):
             ky = lax.axis_index("fft") * rows + i * 2 + k
@@ -559,7 +578,7 @@
             keep = kxz + jnp.full((1, half), ky * ky, jnp.int32).astype(f32) <= bound * bound
             for p in range(2):
                 value = moved[p * length:(p + 1) * length, k * half:(k + 1) * half]
-                done[p, 2 * i + k] = base[p, 2 * i + k] + jnp.where(keep, -0.5 * step_size * value, 0.0)
+                done[p, 2 * i + k] = partial[p, 2 * i + k] + jnp.where(keep, -0.5 * step_size * value, 0.0)
         done_copy(i).start()
 
     each(pair)
@@ -573,6 +592,7 @@
     sides = n // 2
     nch = rows // CHUNK
     groups = rows // 4
+    kinds = 3 + groups - groups // 2
     f32, bf16 = jnp.float32, jnp.bfloat16
     tables = lax.optimization_barrier(build_tables(length, n, rows))
     vmem = pl.BlockSpec(memory_space=pltpu.VMEM)
@@ -581,8 +601,6 @@
     dma = pltpu.SemaphoreType.DMA
     scratch = [pltpu.VMEM(t.shape, bf16) for t in tables] + [
         pltpu.VMEM((4, length, length), bf16),
-        pltpu.VMEM((2, rows, length, half), f32),
-        pltpu.VMEM((rows // 2, 2 * length, 2 * half), bf16),
         pltpu.VMEM((2, rows, 2, length, half), bf16),
         pltpu.VMEM((2, nch, sides, rows, 2 * CHUNK, 2 * half), bf16),
         pltpu.VMEM((sides, 2, nch, rows, 2 * CHUNK, 2 * half), bf16),
@@ -599,42 +617,42 @@
         pltpu.VMEM((2, 8, half), f32),
         pltpu.VMEM((8, 128), f32),
         pltpu.VMEM((n, 8, 128), f32),
-        dma((nch,)), dma((len(tables),)), dma, dma, dma, dma((nch,)), dma((3,)), dma((3,)), dma, dma, dma,
+        dma((nch,)), dma((len(tables),)), dma, dma((nch,)), dma((kinds,)), dma((kinds,)), dma, dma, dma,
         dma((2, n)), dma((2, groups, 2)), dma, dma,
         pltpu.SemaphoreType.REGULAR,
     ]
-    spread, partial, kappa = pl.pallas_call(
+    partial, lined, kappa = pl.pallas_call(
         functools.partial(step_kernel, n, m, rows, length // 3),
         out_shape=[
-            jax.ShapeDtypeStruct((rows // 2, 2 * length, 2 * half), bf16),
-            jax.ShapeDtypeStruct((2, rows, length, half), f32),
-            jax.ShapeDtypeStruct((8, 128), f32),
+            pltpu.VMEM((2, rows, length, half), f32),
+            pltpu.VMEM((rows // 2, 2 * length, 2 * half), bf16),
+            pltpu.VMEM((8, 128), f32),
         ],
         in_specs=[hbm, hbm, smem, smem, smem] + [hbm] * 6,
-        out_specs=[hbm, hbm, vmem],
+        out_specs=[vmem, vmem, vmem],
         scratch_shapes=scratch,
         compiler_params=pltpu.CompilerParams(
-            collective_id=0, has_side_effects=True, vmem_limit_bytes=63 * 1024 * 1024,
+            collective_id=0, has_side_effects=True, vmem_limit_bytes=56 * 1024 * 1024,
         ),
         name="whole_step",
     )(scalar_state[0], velocity, species, kappa_table, dealias_bound, *tables)
+    keep = functools.partial(pltpu.with_memory_space_constraint, memory_space=pltpu.VMEM)
     new_state, kappa = pl.pallas_call(
         functools.partial(final_kernel, rows, length),
         out_shape=[
             jax.ShapeDtypeStruct((2, rows, length, half), f32),
             jax.ShapeDtypeStruct((1,), f32),
         ],
-        in_specs=[hbm, hbm, smem, smem, hbm],
+        in_specs=[vmem, vmem, vmem, smem, hbm],
         out_specs=[hbm, smem],
         scratch_shapes=[
             pltpu.VMEM((2 * length, 2 * length), bf16),
-            pltpu.VMEM((rows // 2, 2 * length, 2 * half), bf16),
             pltpu.VMEM((2, rows, length, half), f32),
-            pltpu.VMEM((2, rows, length, half), f32),
-            dma, dma((rows // 2,)), dma((rows // 2,)), dma((rows // 2,)),
+            dma, dma((rows // 2,)),
         ],
+        compiler_params=pltpu.CompilerParams(vmem_limit_bytes=24 * 1024 * 1024),
         name="final_step",
-    )(spread, partial, kappa, dealias_bound, tables[5])
+    )(keep(partial), keep(lined), keep(kappa), dealias_bound, tables[5])
     return new_state[None], kappa
 
 

time: 230 us -> 223 us (0.970)
  Pallas kernels: 228 us -> 221 us
    pallas_call x1, Pallas kernels: 221 us -> 217 us  [body(): pl.pallas_call(functools.partial(step_kernel, n, m, rows, length // 3), o...]
    pallas_call x1, Pallas kernels: 6.25 us -> 3.73 us  [body(): pl.pallas_call(functools.partial(final_kernel, rows, length), out_shape=[...]
where the time goes in v4:
time: 223 us
  Pallas kernels  221 us (99%)
    pallas_call x1, Pallas kernels, body(): pl.pallas_call(functools.partial(step_kernel, n, m, rows, length // 3), o...  217 us

profile of v4, /device:TPU:0, one launch (start us, length us, event | category | flops | bytes accessed | tf_op | source)
XLA Modules:
  0.0 223.1 jit_solution(4515099493627124590)
XLA Ops:
  1.9 0.0 copy-start
  1.9 217.3 %whole_step.1 = (f32[2,16,256,128]{3,2,1,0:T(8,128)S(1)}, bf16[8,512,256]{2,1,0:T(8,128)(2,1)S(1)}, f32[8,128]{1,0:T(8,128)S(1)}) custom-call(f32[2,16,256,128]{3,2,1,0:T(8,128)} %bitcast.2, bf16[3,16,128,256]{3,2,1,0:T(8,128)(2,1)} %refs_1_.1, s32[1]{0:T(128)S(6)} %copy.13.refs_2_, f32[64]{0:T(128)} %refs_3_.1, s32[1]{0:T(128)S(6)} %copy.14.refs_4_.bounds, ...), custom_call_target="tpu_custom_call" | custom-call | tf_op jit(solution)/shard_map/whole_step/pallas_call | solution.py:624
  219.2 0.0 copy-done
  219.2 3.7 %final_step.1 = (f32[2,16,256,128]{3,2,1,0:T(8,128)}, f32[1]{0:T(128)}) custom-call(f32[2,16,256,128]{3,2,1,0:T(8,128)S(1)} %get-tuple-element.19.partial, bf16[8,512,256]{2,1,0:T(8,128)(2,1)S(1)} %get-tuple-element.20.lined, f32[8,128]{1,0:T(8,128)S(1)} %get-tuple-element.21.kap, s32[1]{0:T(128)S(6)} %copy.14.refs_4_.bounds, bf16[512,512]{1,0:T(8,128)(2,1)S(1)} %copy-done), custom_call_target="tpu_custom_call" | custom-call | tf_op jit(solution)/shard_map/final_step/pallas_call | solution.py:640
Async XLA Ops:
  1.9 217.3 %copy-start = (bf16[512,512]{1,0:T(8,128)(2,1)S(1)}, bf16[512,512]{1,0:T(8,128)(2,1)}, u32[]{:S(2)}) copy-start(bf16[512,512]{1,0:T(8,128)(2,1)} %constant.17.clone.refs_10_.fwd_z_in) | copy-start | bytes 1572868

commit v5 on v4

--- a/solution.py
+++ b/solution.py
@@ -92,7 +92,7 @@
             device_id={"fft": partner}, device_id_type=MESH,
         )
 
-    lower = groups // 2
+    lower = groups - 1
 
     def planes_of(kind):
         if isinstance(kind, int) and kind in (0, 2):
@@ -333,19 +333,12 @@
         else:
             act(d // sides)
 
-    def leave(st, low, high, own, across=None):
+    def leave(st, low, high, own):
         def one(j):
-            d = (me + jnp.where(side == st, j, n - j)) % n
-
-            def send():
-                h = d // sides if own else 1 - d // sides
-                by_tiles(d % sides + h * sides, lambda k: each(
-                    low, high, lambda g: forward_copy(st, g, d, h, me, k).start()))
-
-            if across is None:
-                send()
-            else:
-                pl.when((d // sides != side) if across else (d // sides == side))(send)
+            d = (me + jnp.where(side == 0, j, n - j)) % n
+            h = d // sides if own else 1 - d // sides
+            by_tiles(d % sides + h * sides, lambda k: each(
+                low, high, lambda g: forward_copy(st, g, d, h, me, k).start()))
 
         each(1, n, one)
 
@@ -435,23 +428,12 @@
     local_grad = jnp.sum(acc[1], keepdims=True) / cells
     stat[...] = jnp.where(line == 0, local_var, jnp.where(line == 1, local_grad, largest))
     each(1, n, lambda j: stat_copy((me + j) % n, me).start())
-    leave(0, 2, min(3, groups), True)
-    outer = (place < sides // 2) == (side == 0)
-
-    @pl.when(outer)
-    def _():
-        leave(0, min(3, groups), groups, True)
-        leave(0, 0, groups, False)
-
+    leave(0, 2, groups, True)
+    leave(0, 0, groups, False)
     stats[me] = stat[...]
     rows_sent(0)
     rows_sent(1)
     await_bytes(stats.at[pl.ds(0, n - 1)], t_recv)
-    @pl.when(jnp.logical_not(outer))
-    def _():
-        leave(0, min(3, groups), groups, True)
-        leave(0, 0, groups, False, False)
-
     summed = jnp.sum(stats[...], axis=0)
     highest = jnp.max(stats[...], axis=0)
     kappa = ktable[species[0]] * highest[2:3, :1] * jnp.sqrt(summed[0:1, :1]) / (summed[1:2, :1] + 1e-06)
@@ -502,11 +484,7 @@
         chunks(own, False)
     for own in (True, False):
         unpack(0, side if own else 1 - side)
-        if own:
-            @pl.when(jnp.logical_not(outer))
-            def _():
-                leave(0, 0, groups, False, True)
-        else:
+        if not own:
             each(1, n, lambda j: pl.semaphore_signal(
                 free, inc=1, device_id={"fft": (me + j) % n}, device_id_type=MESH))
         chunks(own, True)
@@ -553,7 +531,7 @@
             act(i)
             return carry
 
-        lax.fori_loop(0, pairs, one, 0, unroll=2)
+        lax.fori_loop(0, pairs, one, 0, unroll=4)
 
     def done_copy(i):
         at = pl.ds(2 * i, 2)
@@ -592,7 +570,7 @@
     sides = n // 2
     nch = rows // CHUNK
     groups = rows // 4
-    kinds = 3 + groups - groups // 2
+    kinds = 4
     f32, bf16 = jnp.float32, jnp.bfloat16
     tables = lax.optimization_barrier(build_tables(length, n, rows))
     vmem = pl.BlockSpec(memory_space=pltpu.VMEM)

time: 223 us -> 221 us (level)
  Pallas kernels: 221 us -> 218 us
    pallas_call x1, Pallas kernels: 217 us -> 215 us  [body(): pl.pallas_call(functools.partial(step_kernel, n, m, rows, length // 3), o...]
where the time goes in v5:
time: 221 us
  Pallas kernels  218 us (99%)
    pallas_call x1, Pallas kernels, body(): pl.pallas_call(functools.partial(step_kernel, n, m, rows, length // 3), o...  215 us

profile of v5, /device:TPU:0, one launch (start us, length us, event | category | flops | bytes accessed | tf_op | source)
XLA Modules:
  0.0 220.6 jit_solution(14252802880638410822)
XLA Ops:
  1.9 0.0 copy-start
  1.9 215.0 %whole_step.1 = (f32[2,16,256,128]{3,2,1,0:T(8,128)S(1)}, bf16[8,512,256]{2,1,0:T(8,128)(2,1)S(1)}, f32[8,128]{1,0:T(8,128)S(1)}) custom-call(f32[2,16,256,128]{3,2,1,0:T(8,128)} %bitcast.2, bf16[3,16,128,256]{3,2,1,0:T(8,128)(2,1)} %refs_1_.1, s32[1]{0:T(128)S(6)} %copy.13.refs_2_, f32[64]{0:T(128)} %refs_3_.1, s32[1]{0:T(128)S(6)} %copy.14.refs_4_.bounds, ...), custom_call_target="tpu_custom_call" | custom-call | tf_op jit(solution)/shard_map/whole_step/pallas_call | solution.py:602
  216.9 0.0 copy-done
  216.9 3.5 %final_step.1 = (f32[2,16,256,128]{3,2,1,0:T(8,128)}, f32[1]{0:T(128)}) custom-call(f32[2,16,256,128]{3,2,1,0:T(8,128)S(1)} %get-tuple-element.19.partial, bf16[8,512,256]{2,1,0:T(8,128)(2,1)S(1)} %get-tuple-element.20.lined, f32[8,128]{1,0:T(8,128)S(1)} %get-tuple-element.21.kap, s32[1]{0:T(128)S(6)} %copy.14.refs_4_.bounds, bf16[512,512]{1,0:T(8,128)(2,1)S(1)} %copy-done), custom_call_target="tpu_custom_call" | custom-call | tf_op jit(solution)/shard_map/final_step/pallas_call | solution.py:618
Async XLA Ops:
  1.9 215.0 %copy-start = (bf16[512,512]{1,0:T(8,128)(2,1)S(1)}, bf16[512,512]{1,0:T(8,128)(2,1)}, u32[]{:S(2)}) copy-start(bf16[512,512]{1,0:T(8,128)(2,1)} %constant.17.clone.refs_10_.fwd_z_in) | copy-start | bytes 1572868

commit v6 on v5

--- a/solution.py
+++ b/solution.py
@@ -531,7 +531,7 @@
             act(i)
             return carry
 
-        lax.fori_loop(0, pairs, one, 0, unroll=4)
+        lax.fori_loop(0, pairs, one, 0, unroll=True)
 
     def done_copy(i):
         at = pl.ds(2 * i, 2)

time: 221 us -> 221 us (level)
  no operation moved by 1% of the time
where the time goes in v6:
time: 221 us; the launch traced here: 220 us
  Pallas kernels  218 us (99%)
    pallas_call x1, Pallas kernels, body(): pl.pallas_call(functools.partial(step_kernel, n, m, rows, length // 3), o...  215 us

profile of v6, /device:TPU:0, one launch (start us, length us, event | category | flops | bytes accessed | tf_op | source)
XLA Modules:
  0.0 220.4 jit_solution(9682422752418583940)
XLA Ops:
  1.9 0.0 copy-start
  1.9 215.0 %whole_step.1 = (f32[2,16,256,128]{3,2,1,0:T(8,128)S(1)}, bf16[8,512,256]{2,1,0:T(8,128)(2,1)S(1)}, f32[8,128]{1,0:T(8,128)S(1)}) custom-call(f32[2,16,256,128]{3,2,1,0:T(8,128)} %bitcast.2, bf16[3,16,128,256]{3,2,1,0:T(8,128)(2,1)} %refs_1_.1, s32[1]{0:T(128)S(6)} %copy.13.refs_2_, f32[64]{0:T(128)} %refs_3_.1, s32[1]{0:T(128)S(6)} %copy.14.refs_4_.bounds, ...), custom_call_target="tpu_custom_call" | custom-call | tf_op jit(solution)/shard_map/whole_step/pallas_call | solution.py:602
  216.9 0.0 copy-done
  216.9 3.3 %final_step.1 = (f32[2,16,256,128]{3,2,1,0:T(8,128)}, f32[1]{0:T(128)}) custom-call(f32[2,16,256,128]{3,2,1,0:T(8,128)S(1)} %get-tuple-element.19.partial, bf16[8,512,256]{2,1,0:T(8,128)(2,1)S(1)} %get-tuple-element.20.lined, f32[8,128]{1,0:T(8,128)S(1)} %get-tuple-element.21.kap, s32[1]{0:T(128)S(6)} %copy.14.refs_4_.bounds, bf16[512,512]{1,0:T(8,128)(2,1)S(1)} %copy-done), custom_call_target="tpu_custom_call" | custom-call | tf_op jit(solution)/shard_map/final_step/pallas_call | solution.py:618
Async XLA Ops:
  1.9 215.0 %copy-start = (bf16[512,512]{1,0:T(8,128)(2,1)S(1)}, bf16[512,512]{1,0:T(8,128)(2,1)}, u32[]{:S(2)}) copy-start(bf16[512,512]{1,0:T(8,128)(2,1)} %constant.17.clone.refs_10_.fwd_z_in) | copy-start | bytes 1572868
